TPU v7x, 32 devices: a whole 2x2x4 slice. The times are simulated.
32 devices in a mesh: rows: 16 (over z, y, x), tp: 2 (over core).
Axes of the slice: x: 2, y: 2, z: 4, core: 2. Of those that a mesh axis runs over, the one named last changes fastest.
Arguments:
- block_input: float32 [512, 16, 768], P('tp', 'rows'), may hold values from -6 to 6
- cotangent: float32 [512, 16, 768], P('tp', 'rows'), may hold values from -6 to 6
- qkv_weight: float32 [2, 768, 3, 768], P(None, 'rows', None, 'tp'), may hold values from -0.21875 to 0.21875
- proj_weight: float32 [2, 768, 768], P(None, 'tp', 'rows'), may hold values from -0.875 to 0.875
- fc1_weight: float32 [2, 768, 3072], P(None, 'rows', 'tp'), may hold values from -0.21875 to 0.21875
- fc2_weight: float32 [2, 3072, 768], P(None, 'tp', 'rows'), may hold values from -0.109375 to 0.109375
- norm_gains: float32 [2, 2, 768], P(None, None, ('rows', 'tp')), may hold values from 0.5 to 1.5
- biases: float32 [2, 6, 768], P(None, None, ('rows', 'tp')), may hold values from -1.75 to 1.75
- fc1_bias: float32 [2, 3072], P(None, ('rows', 'tp')), may hold values from -1.75 to 1.75
- segments: int32 [16, 512], P('rows'), may hold values from 0 to 7, never falling along the last dimension, each value on 1 to 198 neighbouring positions
- keep_flags: int32 [2, 2, 16, 8], P(None, None, 'rows'), may hold values 0 or 1
Outputs:
- block_output: float32 [512, 16, 768], P('tp', 'rows')
- input_grad: float32 [512, 16, 768], P('tp', 'rows')
- query_key_value_gradient: float32 [2, 768, 3, 768], P(None, 'rows', None, 'tp')
- proj_grad: float32 [2, 768, 768], P(None, 'tp', 'rows')
- expand_weight_gradient: float32 [2, 768, 3072], P(None, 'rows', 'tp')
- fc2_grad: float32 [2, 3072, 768], P(None, 'tp', 'rows')
- gains_grad: float32 [2, 2, 768], P(None, None, ('rows', 'tp'))
- biases_grad: float32 [2, 6, 768], P(None, None, ('rows', 'tp'))
- fc1_bias_grad: float32 [2, 3072], P(None, ('rows', 'tp'))
Inputs may be any that keep to these rules, and one draw needn't show every extreme that they name: `segments`: along each packed row the image numbers never decrease; each of the 8 images of a row has 1 to 198 positions, and some image has exactly 198.
All inputs are finite; a program needn't handle non-finite values. No bound on the sum of `keep_flags` on one device may be relied on, other than what follows from the above.
Results may differ from a plain program's by a relative error of at most 0.035.
Values may be sent and summed in bfloat16 or wider, within the bound.
A program may use at most 192 MiB of HBM per device.

v0:
```python
import math

import jax
import jax.numpy as jnp
from jax import lax
from jax.sharding import PartitionSpec as P

HEAD_DIM = 64
LAYERS = 2
SEGS = 8


NORM_EPS = 1e-06
KEEP_RATE = 0.9
SCORE_SCALE = 0.125
MASK_FILL = -1e30
INV_SQRT_TWO = 1.0 / math.sqrt(2.0)
INV_SQRT_TWO_PI = 1.0 / math.sqrt(2.0 * math.pi)


def apply_layer_norm(residual_rows):
    center = residual_rows - jnp.mean(residual_rows, axis=-1, keepdims=True)
    spread = jnp.mean(center * center, axis=-1, keepdims=True)
    inverse_deviation = lax.rsqrt(spread + NORM_EPS)
    return (center * inverse_deviation, inverse_deviation)


def norm_backward(normed_gradient, centered_unit, inverse_deviation, norm_gain):
    scaled_rows = normed_gradient * norm_gain
    return inverse_deviation * (
        scaled_rows
        - jnp.mean(scaled_rows, axis=-1, keepdims=True)
        - centered_unit * jnp.mean(scaled_rows * centered_unit, axis=-1, keepdims=True)
    )


def gelu_slope(hidden_before_gelu):
    return (
        0.5 * (1.0 + lax.erf(hidden_before_gelu * INV_SQRT_TWO))
        + hidden_before_gelu
        * jnp.exp(-0.5 * hidden_before_gelu * hidden_before_gelu)
        * INV_SQRT_TWO_PI
    )


def per_device(
    block_input,
    cotangent,
    qkv_weight,
    proj_weight,
    fc1_weight,
    fc2_weight,
    norm_gains,
    biases,
    fc1_bias,
    segments,
    keep_flags,
):
    local_len, row_count, width = block_input.shape
    tp_rank = lax.axis_index("tp")
    head_cols = qkv_weight.shape[3]
    ff_cols = fc1_weight.shape[2]
    head_count = head_cols // HEAD_DIM
    first_token = tp_rank * local_len
    same_image = segments[:, :, None] == segments[:, None, :]
    local_segments = lax.dynamic_slice_in_dim(segments, first_token, local_len, 1)
    member = (
        local_segments[:, :, None] == jnp.arange(SEGS, dtype=jnp.int32)[None, None, :]
    ).astype(jnp.float32)

    def token_keep(keep_row):
        picked = jnp.sum(member * keep_row.astype(jnp.float32)[:, None, :], axis=2)
        return jnp.transpose(picked)[:, :, None]

    def place(part_grad, total_len):
        return lax.dynamic_update_slice_in_dim(
            jnp.zeros((total_len,), jnp.float32), part_grad, tp_rank * part_grad.shape[0], 0
        )

    def project_in(normed_rows, weight, norm_shift):
        return (
            jnp.einsum(
                "trd,dc->trc",
                lax.all_gather(normed_rows, "tp", axis=0, tiled=True),
                weight,
                preferred_element_type=jnp.float32,
            )
            + norm_shift,
            None,
        )

    def project_out(full_rows, weight):

        def partial_term(first_row, row_span):
            return jnp.einsum("trc,cd->trd", full_rows, weight, preferred_element_type=jnp.float32)

        return lax.psum_scatter(
            partial_term(jnp.int32(0), local_len * lax.axis_size("tp")).astype(jnp.bfloat16),
            "tp",
            scatter_dimension=0,
            tiled=True,
        ).astype(jnp.float32)

    def project_back(full_grads, weight):

        def partial_term(first_row, row_span):
            return jnp.einsum("trc,dc->trd", full_grads, weight, preferred_element_type=jnp.float32)

        return lax.psum_scatter(
            partial_term(jnp.int32(0), local_len * lax.axis_size("tp")).astype(jnp.bfloat16),
            "tp",
            scatter_dimension=0,
            tiled=True,
        ).astype(jnp.float32)

    def gathered_grads(gradient_reduced, kept_side, weight):
        shard_part = lax.all_gather(gradient_reduced, "tp", axis=0, tiled=True)
        weight_sum = jnp.einsum(
            "trc,trd->cd", kept_side, shard_part, preferred_element_type=jnp.float32
        )
        fresh = jnp.einsum("trd,cd->trc", shard_part, weight, preferred_element_type=jnp.float32)
        return (weight_sum, fresh)

    def input_weight_gradient(centered_unit, norm_gain, norm_shift, gradient_reduced):
        normed_rows = (centered_unit * norm_gain + norm_shift).astype(jnp.bfloat16)
        return jnp.einsum(
            "trd,trc->dc",
            lax.all_gather(normed_rows, "tp", axis=0, tiled=True),
            gradient_reduced,
            preferred_element_type=jnp.float32,
        )

    def attention_scores(queries_low, keys_low):
        scores = (
            jnp.einsum("qrhd,krhd->rhqk", queries_low, keys_low, preferred_element_type=jnp.float32)
            * SCORE_SCALE
        )
        return jnp.where(same_image[:, None], scores, MASK_FILL)

    residual_rows = block_input
    saved = []
    for layer_position in range(LAYERS):
        qkv_low = qkv_weight[layer_position].astype(jnp.bfloat16)
        proj_low = proj_weight[layer_position].astype(jnp.bfloat16)
        fc1_low = fc1_weight[layer_position].astype(jnp.bfloat16)
        fc2_low = fc2_weight[layer_position].astype(jnp.bfloat16)
        weights = (
            lax.all_gather(qkv_low, "rows", axis=0, tiled=True),
            lax.all_gather(proj_low, "rows", axis=1, tiled=True),
            lax.all_gather(fc1_low, "rows", axis=0, tiled=True),
            lax.all_gather(fc2_low, "rows", axis=1, tiled=True),
        )
        vectors = (
            lax.all_gather(norm_gains[layer_position], ("rows", "tp"), axis=1, tiled=True),
            lax.all_gather(biases[layer_position], ("rows", "tp"), axis=1, tiled=True),
            lax.all_gather(fc1_bias[layer_position], ("rows", "tp"), axis=0, tiled=True),
        )
        w_qkv, w_proj, w_fc1, w_fc2 = weights
        gain_row_block, bias_row_block, fc1_full = vectors
        w_joined = w_qkv.reshape(width, 3 * head_cols)
        query_bias = lax.dynamic_slice_in_dim(bias_row_block[1], tp_rank * head_cols, head_cols, 0)
        value_bias = lax.dynamic_slice_in_dim(bias_row_block[2], tp_rank * head_cols, head_cols, 0)
        in_bias = jnp.concatenate([query_bias, jnp.zeros((head_cols,), jnp.float32), value_bias])
        fc1_local = lax.dynamic_slice_in_dim(fc1_full, tp_rank * ff_cols, ff_cols, 0)
        keep_attn = token_keep(keep_flags[layer_position, 0])
        keep_mlp = token_keep(keep_flags[layer_position, 1])
        first_centered_unit, first_inverse_deviation = apply_layer_norm(residual_rows)
        first_normed_rows = (first_centered_unit * gain_row_block[0] + bias_row_block[0]).astype(
            jnp.bfloat16
        )
        projected, whole_one = project_in(first_normed_rows, w_joined, in_bias)
        joined_low = projected.astype(jnp.bfloat16)
        full_len = joined_low.shape[0]
        queries_low = joined_low[:, :, :head_cols].reshape(
            full_len, row_count, head_count, HEAD_DIM
        )
        keys_low = joined_low[:, :, head_cols : 2 * head_cols].reshape(
            full_len, row_count, head_count, HEAD_DIM
        )
        values_low = joined_low[:, :, 2 * head_cols :].reshape(
            full_len, row_count, head_count, HEAD_DIM
        )
        scores = attention_scores(queries_low, keys_low)
        row_top = jnp.max(scores, axis=-1, keepdims=True)
        exponent = jnp.exp(scores - row_top)
        row_total = jnp.sum(exponent, axis=-1, keepdims=True)
        log_total = row_top + jnp.log(row_total)
        probs_low = (exponent / row_total).astype(jnp.bfloat16)
        context = jnp.einsum(
            "rhqk,krhd->qrhd", probs_low, values_low, preferred_element_type=jnp.float32
        )
        context_low = context.reshape(full_len, row_count, head_cols).astype(jnp.bfloat16)
        attn = project_out(context_low, w_proj) + bias_row_block[3]
        middle_residual = residual_rows + keep_attn * attn / KEEP_RATE
        second_centered_unit, second_inverse_deviation = apply_layer_norm(middle_residual)
        second_normed_rows = (second_centered_unit * gain_row_block[1] + bias_row_block[4]).astype(
            jnp.bfloat16
        )
        hidden_before_gelu, whole_two = project_in(second_normed_rows, w_fc1, fc1_local)
        hidden_low = jax.nn.gelu(hidden_before_gelu, approximate=False).astype(jnp.bfloat16)
        feedforward_block = project_out(hidden_low, w_fc2) + bias_row_block[5]
        residual_rows = middle_residual + keep_mlp * feedforward_block / KEEP_RATE
        saved.append(
            (
                first_centered_unit,
                first_inverse_deviation,
                second_centered_unit,
                second_inverse_deviation,
                queries_low,
                keys_low,
                values_low,
                log_total,
                context_low,
                hidden_before_gelu,
                whole_one,
                whole_two,
                weights,
                vectors,
                keep_attn,
                keep_mlp,
            )
        )
    residual_gradient = cotangent
    qkv_list = [None] * LAYERS
    proj_list = [None] * LAYERS
    fc1_list = [None] * LAYERS
    fc2_list = [None] * LAYERS
    gain_list = [None] * LAYERS
    bias_list = [None] * LAYERS
    fc1_bias_list = [None] * LAYERS
    for layer_position in reversed(range(LAYERS)):
        (
            first_centered_unit,
            first_inverse_deviation,
            second_centered_unit,
            second_inverse_deviation,
            queries_low,
            keys_low,
            values_low,
            log_total,
            context_low,
            hidden_before_gelu,
            whole_one,
            whole_two,
            kept_weights,
            vectors,
            keep_attn,
            keep_mlp,
        ) = saved[layer_position]
        qkv_again = qkv_weight[layer_position].astype(jnp.bfloat16)
        proj_again = proj_weight[layer_position].astype(jnp.bfloat16)
        fc1_again = fc1_weight[layer_position].astype(jnp.bfloat16)
        fc2_again = fc2_weight[layer_position].astype(jnp.bfloat16)
        weights = (
            lax.all_gather(qkv_again, "rows", axis=0, tiled=True),
            lax.all_gather(proj_again, "rows", axis=1, tiled=True),
            lax.all_gather(fc1_again, "rows", axis=0, tiled=True),
            lax.all_gather(fc2_again, "rows", axis=1, tiled=True),
        )
        w_qkv, w_proj, w_fc1, w_fc2 = weights
        gain_row_block, bias_row_block, fc1_full = vectors
        w_joined = w_qkv.reshape(width, 3 * head_cols)
        full_len = queries_low.shape[0]
        mlp_grad = residual_gradient * keep_mlp / KEEP_RATE
        fc2_bias_grad = jnp.sum(mlp_grad, axis=(0, 1))
        hidden_low = jax.nn.gelu(hidden_before_gelu, approximate=False).astype(jnp.bfloat16)
        fc2_grad, hidden_grad = gathered_grads(mlp_grad.astype(jnp.bfloat16), hidden_low, w_fc2)
        preactivation_gradient = (hidden_grad * gelu_slope(hidden_before_gelu)).astype(jnp.bfloat16)
        fc1_bias_local = jnp.sum(preactivation_gradient.astype(jnp.float32), axis=(0, 1))
        expand_weight_gradient = input_weight_gradient(
            second_centered_unit, gain_row_block[1], bias_row_block[4], preactivation_gradient
        )
        second_gradient = project_back(preactivation_gradient, w_fc1)
        second_norm_gain = jnp.sum(second_gradient * second_centered_unit, axis=(0, 1))
        shift_two = jnp.sum(second_gradient, axis=(0, 1))
        middle_gradient = residual_gradient + norm_backward(
            second_gradient, second_centered_unit, second_inverse_deviation, gain_row_block[1]
        )
        attn_grad = middle_gradient * keep_attn / KEEP_RATE
        proj_bias_grad = jnp.sum(attn_grad, axis=(0, 1))
        proj_grad, context_grad = gathered_grads(
            attn_grad.astype(jnp.bfloat16), context_low, w_proj
        )
        context_grad_low = context_grad.astype(jnp.bfloat16).reshape(
            full_len, row_count, head_count, HEAD_DIM
        )
        scores = attention_scores(queries_low, keys_low)
        probabilities = jnp.exp(scores - log_total)
        probs_low = probabilities.astype(jnp.bfloat16)
        value_grad = jnp.einsum(
            "rhqk,qrhd->krhd", probs_low, context_grad_low, preferred_element_type=jnp.float32
        )
        prob_grad = jnp.einsum(
            "qrhd,krhd->rhqk", context_grad_low, values_low, preferred_element_type=jnp.float32
        )
        row_delta = jnp.sum(prob_grad * probabilities, axis=-1, keepdims=True)
        score_grad = (probabilities * (prob_grad - row_delta)).astype(jnp.bfloat16)
        query_grad = (
            jnp.einsum("rhqk,krhd->qrhd", score_grad, keys_low, preferred_element_type=jnp.float32)
            * SCORE_SCALE
        )
        key_grad = (
            jnp.einsum(
                "rhqk,qrhd->krhd", score_grad, queries_low, preferred_element_type=jnp.float32
            )
            * SCORE_SCALE
        )
        combined_gradient = jnp.concatenate(
            [
                query_grad.reshape(full_len, row_count, head_cols),
                key_grad.reshape(full_len, row_count, head_cols),
                value_grad.reshape(full_len, row_count, head_cols),
            ],
            axis=2,
        ).astype(jnp.bfloat16)
        in_bias_grad = jnp.sum(combined_gradient.astype(jnp.float32), axis=(0, 1))
        query_key_value_gradient = input_weight_gradient(
            first_centered_unit, gain_row_block[0], bias_row_block[0], combined_gradient
        )
        first_gradient = project_back(combined_gradient, w_joined)
        first_norm_gain = jnp.sum(first_gradient * first_centered_unit, axis=(0, 1))
        shift_one = jnp.sum(first_gradient, axis=(0, 1))
        residual_gradient = middle_gradient + norm_backward(
            first_gradient, first_centered_unit, first_inverse_deviation, gain_row_block[0]
        )
        gain_grads = jnp.stack([first_norm_gain, second_norm_gain])
        bias_grads = jnp.stack(
            [
                shift_one,
                place(in_bias_grad[:head_cols], width),
                place(in_bias_grad[2 * head_cols :], width),
                proj_bias_grad,
                shift_two,
                fc2_bias_grad,
            ]
        )
        fc1_bias_full = place(fc1_bias_local, fc1_full.shape[0])
        vector_sums = (
            lax.psum_scatter(gain_grads, ("rows", "tp"), scatter_dimension=1, tiled=True),
            lax.psum_scatter(bias_grads, ("rows", "tp"), scatter_dimension=1, tiled=True),
            lax.psum_scatter(fc1_bias_full, ("rows", "tp"), scatter_dimension=0, tiled=True),
        )
        gain_list[layer_position] = vector_sums[0]
        bias_list[layer_position] = vector_sums[1]
        fc1_bias_list[layer_position] = vector_sums[2]
        weight_sums = (
            lax.psum_scatter(
                query_key_value_gradient.reshape(width, 3, head_cols),
                "rows",
                scatter_dimension=0,
                tiled=True,
            ),
            lax.psum_scatter(proj_grad, "rows", scatter_dimension=1, tiled=True),
            lax.psum_scatter(expand_weight_gradient, "rows", scatter_dimension=0, tiled=True),
            lax.psum_scatter(fc2_grad, "rows", scatter_dimension=1, tiled=True),
        )
        qkv_list[layer_position] = weight_sums[0]
        proj_list[layer_position] = weight_sums[1]
        fc1_list[layer_position] = weight_sums[2]
        fc2_list[layer_position] = weight_sums[3]
    qkv_out = jnp.stack(qkv_list)
    proj_out = jnp.stack(proj_list)
    fc1_out = jnp.stack(fc1_list)
    fc2_out = jnp.stack(fc2_list)
    return (
        residual_rows,
        residual_gradient,
        qkv_out,
        proj_out,
        fc1_out,
        fc2_out,
        jnp.stack(gain_list),
        jnp.stack(bias_list),
        jnp.stack(fc1_bias_list),
    )


def solution(mesh):
    placed = (
        P("tp", "rows", None),
        P("tp", "rows", None),
        P(None, "rows", None, "tp"),
        P(None, "tp", "rows"),
        P(None, "rows", "tp"),
        P(None, "tp", "rows"),
        P(None, None, ("rows", "tp")),
        P(None, None, ("rows", "tp")),
        P(None, ("rows", "tp")),
        P("rows", None),
        P(None, None, "rows", None),
    )
    return jax.shard_map(
        per_device,
        mesh=mesh,
        in_specs=placed,
        out_specs=(
            P("tp", "rows", None),
            P("tp", "rows", None),
            P(None, "rows", None, "tp"),
            P(None, "tp", "rows"),
            P(None, "rows", "tp"),
            P(None, "tp", "rows"),
            P(None, None, ("rows", "tp")),
            P(None, None, ("rows", "tp")),
            P(None, ("rows", "tp")),
        ),
        check_vma=False,
    )
```

profile of v0, /device:TPU:0, one launch (start us, length us, event | category | flops | bytes accessed | tf_op | source)
XLA Modules:
  0.0 1991.3 jit_solution(3101226865566057588)
XLA Ops:
  13.9 44.4 %all-gather = f32[1,2,768]{1,0,2:T(1,128)S(1)} all-gather(f32[1,2,24]{1,0,2:T(1,128)S(1)} %copy.180), channel_id=2, replica_groups=mesh['rows'=16,'tp'=2] {'rows','tp'}, dimensions={2}, use_global_device_ids=true | all-gather | bytes 6336 | tf_op jit(solution)/shard_map/all_gather | solution.py:154
  58.3 37.9 %all-gather.1 = f32[1,6,768]{1,0,2:T(1,128)S(1)} all-gather(f32[1,6,24]{1,0,2:T(1,128)S(1)} %copy.181), channel_id=3, replica_groups=mesh['rows'=16,'tp'=2] {'rows','tp'}, dimensions={2}, use_global_device_ids=true | all-gather | bytes 19008 | tf_op jit(solution)/shard_map/all_gather | solution.py:155
  96.2 39.4 %all-gather.8 = f32[1,6,768]{1,0,2:T(1,128)S(1)} all-gather(f32[1,6,24]{1,0,2:T(1,128)S(1)} %copy.183), channel_id=10, replica_groups=mesh['rows'=16,'tp'=2] {'rows','tp'}, dimensions={2}, use_global_device_ids=true | all-gather | bytes 19008 | tf_op jit(solution)/shard_map/all_gather | solution.py:155
  135.7 15.3 fusion.179
  152.4 14.9 fusion.180
  176.5 38.8 %all-gather.3 = bf16[1,384,768]{1,2,0:T(8,128)(2,1)S(1)} all-gather(bf16[1,384,48]{1,2,0:T(8,128)(2,1)S(1)} %get-tuple-element.134), channel_id=5, replica_groups=mesh['rows'=16,'tp'=2] {'rows'}, dimensions={2}, use_global_device_ids=true | all-gather | bytes 626688 | tf_op jit(solution)/shard_map/all_gather | solution.py:149
  236.0 37.9 %all-reduce.9 = (f32[3072]{0:T(1024)S(1)}, f32[3072]{0:T(1024)S(1)}) all-reduce(f32[3072]{0:T(1024)S(1)} %bitcast_dynamic-update-slice_fusion.1, f32[3072]{0:T(1024)S(1)} %bitcast_dynamic-update-slice_fusion), channel_id=7, replica_groups=mesh['rows'=16,'tp'=2] {'rows','tp'}, use_global_device_ids=true, to_apply=%add | all-reduce | flops 6144 | bytes 49152
  278.3 27.4 %all-gather.23.cloned.1.call-done = bf16[1,768,1536]{2,1,0:T(8,128)(2,1)} async-done(((bf16[1,48,1536]{2,1,0:T(8,128)(2,1)}), bf16[1,768,1536]{2,1,0:T(8,128)(2,1)}) %all-gather.23.cloned.1.call-update) | async-done | bytes 2359312 | tf_op jit(solution)/shard_map/all_gather | solution.py:150
  305.7 10.4 fusion.6
  316.2 53.4 %all-gather.25.cloned.1.call-done = bf16[1,1536,768]{1,2,0:T(8,128)(2,1)} async-done(((bf16[1,1536,48]{1,2,0:T(8,128)(2,1)}), bf16[1,1536,768]{1,2,0:T(8,128)(2,1)}) %all-gather.25.cloned.1.call-update) | async-done | bytes 2359312 | tf_op jit(solution)/shard_map/all_gather | solution.py:151
  374.1 40.2 %all-gather.7 = f32[1,2,768]{1,0,2:T(1,128)S(1)} all-gather(f32[1,2,24]{1,0,2:T(1,128)S(1)} %copy.182), channel_id=9, replica_groups=mesh['rows'=16,'tp'=2] {'rows','tp'}, dimensions={2}, use_global_device_ids=true | all-gather | bytes 6336 | tf_op jit(solution)/shard_map/all_gather | solution.py:154
  419.0 39.8 %all-gather.10 = bf16[1,384,768]{1,2,0:T(8,128)(2,1)S(1)} all-gather(bf16[1,384,48]{1,2,0:T(8,128)(2,1)S(1)} %get-tuple-element.133), channel_id=12, replica_groups=mesh['rows'=16,'tp'=2] {'rows'}, dimensions={2}, use_global_device_ids=true | all-gather | bytes 626688 | tf_op jit(solution)/shard_map/all_gather | solution.py:149
  492.7 61.8 %all-gather.29.cloned.1.call-done = bf16[1,768,1536]{2,1,0:T(8,128)(2,1)} async-done(((bf16[1,48,1536]{2,1,0:T(8,128)(2,1)}), bf16[1,768,1536]{2,1,0:T(8,128)(2,1)}) %all-gather.29.cloned.1.call-update) | async-done | bytes 2359312 | tf_op jit(solution)/shard_map/all_gather | solution.py:150
  554.6 10.5 fusion.9
  565.1 52.9 %all-gather.31.cloned.1.call-done = bf16[1,1536,768]{1,2,0:T(8,128)(2,1)} async-done(((bf16[1,1536,48]{1,2,0:T(8,128)(2,1)}), bf16[1,1536,768]{1,2,0:T(8,128)(2,1)}) %all-gather.31.cloned.1.call-update) | async-done | bytes 2359312 | tf_op jit(solution)/shard_map/all_gather | solution.py:151
  783.5 87.0 %all-reduce.12.cloned.1.call-done = (f32[2,768]{1,0:T(2,128)}, f32[2,768]{1,0:T(2,128)}, f32[6,768]{1,0:T(8,128)}, f32[6,768]{1,0:T(8,128)}, f32[3072]{0:T(1024)}, /*index=5*/f32[3072]{0:T(1024)}) async-done(((f32[2,768]{1,0:T(2,128)}, f32[2,768]{1,0:T(2,128)}, f32[6,768]{1,0:T(8,128)}, f32[6,768]{1,0:T(8,128)}, f32[3072]{0:T(1024)}, /*index=5*/f32[3072]{0:T(1024)}), (f32[2,768]{1,0:T(2,128)}, ...) | async-done | bytes 73744
  876.8 125.4 %reduce-scatter.43.cloned.1.call-done = f32[384,48]{0,1:T(8,128)} async-done(((f32[384,768]{0,1:T(8,128)}), f32[384,48]{0,1:T(8,128)}) %reduce-scatter.43.cloned.1.call-update) | async-done | bytes 73744 | tf_op jit(solution)/shard_map/reduce_scatter | solution.py:353
  1002.2 129.3 %reduce-scatter.41.cloned.1.call-done = f32[384,48]{0,1:T(8,128)} async-done(((f32[384,768]{0,1:T(8,128)}), f32[384,48]{0,1:T(8,128)}) %reduce-scatter.41.cloned.1.call-update) | async-done | bytes 73744 | tf_op jit(solution)/shard_map/reduce_scatter | solution.py:353
  1133.1 137.6 %reduce-scatter.39.cloned.1.call-done = f32[48,3,384]{2,0,1:T(8,128)} async-done(((f32[768,3,384]{2,0,1:T(8,128)}), f32[48,3,384]{2,0,1:T(8,128)}) %reduce-scatter.39.cloned.1.call-update) | async-done | bytes 221200 | tf_op jit(solution)/shard_map/reduce_scatter | solution.py:347
  1270.7 139.4 %reduce-scatter.37.cloned.1.call-done = f32[48,3,384]{2,0,1:T(8,128)} async-done(((f32[768,3,384]{2,0,1:T(8,128)}), f32[48,3,384]{2,0,1:T(8,128)}) %reduce-scatter.37.cloned.1.call-update) | async-done | bytes 221200 | tf_op jit(solution)/shard_map/reduce_scatter | solution.py:347
  1411.9 141.5 %reduce-scatter.51.cloned.1.call-done = f32[1536,48]{0,1:T(8,128)} async-done(((f32[1536,768]{0,1:T(8,128)}), f32[1536,48]{0,1:T(8,128)}) %reduce-scatter.51.cloned.1.call-update) | async-done | bytes 294928 | tf_op jit(solution)/shard_map/reduce_scatter | solution.py:355
  1553.4 143.1 %reduce-scatter.49.cloned.1.call-done = f32[1536,48]{0,1:T(8,128)} async-done(((f32[1536,768]{0,1:T(8,128)}), f32[1536,48]{0,1:T(8,128)}) %reduce-scatter.49.cloned.1.call-update) | async-done | bytes 294928 | tf_op jit(solution)/shard_map/reduce_scatter | solution.py:355
  1698.4 141.2 %reduce-scatter.47.cloned.1.call-done = f32[48,1536]{1,0:T(8,128)} async-done(((f32[768,1536]{1,0:T(8,128)}), f32[48,1536]{1,0:T(8,128)}) %reduce-scatter.47.cloned.1.call-update) | async-done | bytes 294928 | tf_op jit(solution)/shard_map/reduce_scatter | solution.py:354
  1839.6 143.1 %reduce-scatter.45.cloned.1.call-done = f32[48,1536]{1,0:T(8,128)} async-done(((f32[768,1536]{1,0:T(8,128)}), f32[48,1536]{1,0:T(8,128)}) %reduce-scatter.45.cloned.1.call-update) | async-done | bytes 294928 | tf_op jit(solution)/shard_map/reduce_scatter | solution.py:354
  (466 shorter events, 262.8 us)
Async XLA Ops:
  7.2 208.1 %all-gather.21.cloned.1.call-start = ((), (), s32[]{:S(2)}) async-start(), calls=%async_computation.32 | async-start | bytes 1880064 | tf_op jit(solution)/shard_map/all_gather | solution.py:148
  9.0 265.2 %reduce-scatter.21.cloned.1.call-start = ((), (), s32[]{:S(2)}) async-start(), calls=%async_computation.16 | async-start | bytes 1179648 | tf_op jit(solution)/shard_map/reduce_scatter | solution.py:97
  232.3 73.4 %all-gather.23.cloned.1.call-start = ((), (), s32[]{:S(2)}) async-start(), calls=%async_computation.33 | async-start | bytes 2506752 | tf_op jit(solution)/shard_map/all_gather | solution.py:150
  234.2 135.3 %all-gather.25.cloned.1.call-start = ((), (), s32[]{:S(2)}) async-start(), calls=%async_computation.34 | async-start | bytes 2506752 | tf_op jit(solution)/shard_map/all_gather | solution.py:151
  235.1 223.7 %all-gather.27.cloned.1.call-start = ((), (), s32[]{:S(2)}) async-start(), calls=%async_computation.35 | async-start | bytes 1880064 | tf_op jit(solution)/shard_map/all_gather | solution.py:148
  235.7 227.1 %reduce-scatter.23.cloned.1.call-start = ((), (), s32[]{:S(2)}) async-start(), calls=%async_computation.17 | async-start | bytes 1179648 | tf_op jit(solution)/shard_map/reduce_scatter | solution.py:97
  274.1 213.7 %copy-start.98 = (f32[256]{0:T(256)}, f32[256]{0:T(256)S(1)}, u32[]{:S(2)}) copy-start(f32[256]{0:T(256)S(1)} %get-tuple-element.83) | copy-start | bytes 3076
  374.0 113.8 %reduce-scatter.25.cloned.1.call-start = ((), (), s32[]{:S(2)}) async-start(), calls=%async_computation.18 | async-start | bytes 1179648 | tf_op jit(solution)/shard_map/reduce_scatter | solution.py:97
  482.5 72.1 %all-gather.29.cloned.1.call-start = ((), (), s32[]{:S(2)}) async-start(), calls=%async_computation.36 | async-start | bytes 2506752 | tf_op jit(solution)/shard_map/all_gather | solution.py:150
  483.3 134.7 %all-gather.31.cloned.1.call-start = ((), (), s32[]{:S(2)}) async-start(), calls=%async_computation.37 | async-start | bytes 2506752 | tf_op jit(solution)/shard_map/all_gather | solution.py:151
  484.0 149.8 %reduce-scatter.29.cloned.1.call-start = ((), (), s32[]{:S(2)}) async-start(), calls=%async_computation.20 | async-start | bytes 1179648 | tf_op jit(solution)/shard_map/reduce_scatter | solution.py:109
  627.1 18.8 reduce-scatter.27.cloned.1.call-start
  631.7 43.5 %reduce-scatter.31.cloned.1.call-start = ((), (), s32[]{:S(2)}) async-start(), calls=%async_computation.21 | async-start | bytes 1179648 | tf_op jit(solution)/shard_map/reduce_scatter | solution.py:109
  665.7 31.9 %reduce-scatter.33.cloned.1.call-start = ((), (), s32[]{:S(2)}) async-start(), calls=%async_computation.22 | async-start | bytes 1179648 | tf_op jit(solution)/shard_map/reduce_scatter | solution.py:109
  688.1 51.1 %reduce-scatter.35.cloned.1.call-start = ((), (), s32[]{:S(2)}) async-start(), calls=%async_computation.23 | async-start | bytes 1179648 | tf_op jit(solution)/shard_map/reduce_scatter | solution.py:109
  718.9 151.7 %all-reduce.12.cloned.1.call-start = ((), (), s32[]{:S(2)}) async-start(), calls=%async_computation.38 | async-start | bytes 172032
  744.4 257.8 %reduce-scatter.43.cloned.1.call-start = ((), (), s32[]{:S(2)}) async-start(), calls=%async_computation.27 | async-start | bytes 1253376 | tf_op jit(solution)/shard_map/reduce_scatter | solution.py:353
  747.1 384.4 %reduce-scatter.41.cloned.1.call-start = ((), (), s32[]{:S(2)}) async-start(), calls=%async_computation.26 | async-start | bytes 1253376 | tf_op jit(solution)/shard_map/reduce_scatter | solution.py:353
  750.2 520.6 %reduce-scatter.39.cloned.1.call-start = ((), (), s32[]{:S(2)}) async-start(), calls=%async_computation.25 | async-start | bytes 3760128 | tf_op jit(solution)/shard_map/reduce_scatter | solution.py:347
  753.4 656.7 %reduce-scatter.37.cloned.1.call-start = ((), (), s32[]{:S(2)}) async-start(), calls=%async_computation.24 | async-start | bytes 3760128 | tf_op jit(solution)/shard_map/reduce_scatter | solution.py:347
  757.7 795.7 %reduce-scatter.51.cloned.1.call-start = ((), (), s32[]{:S(2)}) async-start(), calls=%async_computation.31 | async-start | bytes 5013504 | tf_op jit(solution)/shard_map/reduce_scatter | solution.py:355
  762.9 933.6 %reduce-scatter.49.cloned.1.call-start = ((), (), s32[]{:S(2)}) async-start(), calls=%async_computation.30 | async-start | bytes 5013504 | tf_op jit(solution)/shard_map/reduce_scatter | solution.py:355
  768.2 1071.5 %reduce-scatter.47.cloned.1.call-start = ((), (), s32[]{:S(2)}) async-start(), calls=%async_computation.29 | async-start | bytes 5013504 | tf_op jit(solution)/shard_map/reduce_scatter | solution.py:354
  773.5 1209.2 %reduce-scatter.45.cloned.1.call-start = ((), (), s32[]{:S(2)}) async-start(), calls=%async_computation.28 | async-start | bytes 5013504 | tf_op jit(solution)/shard_map/reduce_scatter | solution.py:354
  (114 other events, 1751.7 us)
Sparse Core Ops, SparseCore 0:
  11.2 62.4 all-gather.20
  232.5 5.8 reduce-scatter.20
  241.8 63.9 all-gather.22
  308.9 60.5 all-gather.24
  372.7 59.9 all-gather.26
  435.3 6.1 reduce-scatter.22
  482.6 5.1 reduce-scatter.24
  491.2 63.3 all-gather.28
  557.4 60.5 all-gather.30
  627.2 6.5 reduce-scatter.28
  636.6 9.2 reduce-scatter.26
  665.8 9.2 reduce-scatter.30
  688.2 9.2 reduce-scatter.32
  719.0 9.2 reduce-scatter.34
  744.5 125.9 all-reduce.11
  875.2 126.9 reduce-scatter.42
  1006.8 124.6 reduce-scatter.40
  1136.5 134.1 reduce-scatter.38
  1275.8 134.2 reduce-scatter.36
  1415.1 138.2 reduce-scatter.50
  1558.6 137.8 reduce-scatter.48
  1701.7 137.9 reduce-scatter.46
  1844.8 137.8 reduce-scatter.44
where the time goes:
time: 2000 us; the launch traced here: 1990 us
  waiting for transfers between devices  1420 us (71%)
  blocking collectives  299 us (15%)
  local copies, waits for them, and re-layouts  109 us (5%)
  matrix products  103 us (5%)
  other arithmetic  48.9 us (2%)
    reduce_scatter x2, waiting for transfers between devices, per_device(): lax.psum_scatter(fc2_grad, 'rows', scatter_dimension=1, tiled=True)  285 us
    reduce_scatter x2, waiting for transfers between devices, per_device(): lax.psum_scatter(expand_weight_gradient, 'rows', scatter_dimension=0, til...  284 us
    reduce_scatter x2, waiting for transfers between devices, per_device(): lax.psum_scatter(query_key_value_gradient.reshape(width, 3, head_cols), '...  277 us
    reduce_scatter x2, waiting for transfers between devices, per_device(): lax.psum_scatter(proj_grad, 'rows', scatter_dimension=1, tiled=True)  255 us
    all_gather x2, waiting for transfers between devices, per_device(): lax.all_gather(fc2_low, 'rows', axis=1, tiled=True)  106 us
    unnamed x24, waiting for transfers between devices  89.3 us
    all_gather x2, waiting for transfers between devices, per_device(): lax.all_gather(fc1_low, 'rows', axis=0, tiled=True)  89.2 us
    all_gather x2, blocking collectives, per_device(): lax.all_gather(norm_gains[layer_position], ('rows', 'tp'), axis=1, tiled=...  84.7 us
  transfers between devices with their start and end apart: 23, of which 18 were waited for; matrix products, arithmetic and copies ran while one was open for 8% of the time, Pallas kernels for 0%

commit v1 on v0

v1 whole, which is shorter than its diff:
```python
import math

import jax
import jax.numpy as jnp
from jax import lax
from jax.sharding import PartitionSpec as P

HEAD_DIM = 64
LAYERS = 2
SEGS = 8

NORM_EPS = 1e-06
KEEP_RATE = 0.9
SCORE_SCALE = 0.125
MASK_FILL = -1e30
INV_SQRT_TWO = 1.0 / math.sqrt(2.0)
INV_SQRT_TWO_PI = 1.0 / math.sqrt(2.0 * math.pi)


def apply_layer_norm(residual_rows):
    center = residual_rows - jnp.mean(residual_rows, axis=-1, keepdims=True)
    spread = jnp.mean(center * center, axis=-1, keepdims=True)
    inverse_deviation = lax.rsqrt(spread + NORM_EPS)
    return (center * inverse_deviation, inverse_deviation)


def norm_backward(normed_gradient, centered_unit, inverse_deviation, norm_gain):
    scaled_rows = normed_gradient * norm_gain
    return inverse_deviation * (
        scaled_rows
        - jnp.mean(scaled_rows, axis=-1, keepdims=True)
        - centered_unit * jnp.mean(scaled_rows * centered_unit, axis=-1, keepdims=True)
    )


def cumulative(u):
    return 0.5 * (1.0 + lax.erf(u * INV_SQRT_TWO))


def gelu_slope(u):
    return cumulative(u) + u * jnp.exp(-0.5 * u * u) * INV_SQRT_TWO_PI


def mul(a, b, dims):
    return lax.dot_general(a, b, (dims, ((), ())), preferred_element_type=jnp.float32)


def gather_packed(shard):
    return lax.all_gather(shard, "rows", axis=0, tiled=True)


def scatter_packed(partial):
    return lax.psum_scatter(partial, "rows", scatter_dimension=0, tiled=True)


def per_device(
    block_input,
    cotangent,
    qkv_weight,
    proj_weight,
    fc1_weight,
    fc2_weight,
    norm_gains,
    biases,
    fc1_bias,
    segments,
    keep_flags,
):
    local_len, row_count, width = block_input.shape
    assert row_count == 1
    tp_rank = lax.axis_index("tp")
    tp_size = lax.axis_size("tp")
    full_len = local_len * tp_size
    shard_rows = qkv_weight.shape[1]
    head_cols = qkv_weight.shape[3]
    ff_cols = fc1_weight.shape[2]
    head_count = head_cols // HEAD_DIM
    qkv_end = 3 * head_cols
    proj_end = qkv_end + head_cols
    fc1_end = proj_end + ff_cols
    bf16 = jnp.bfloat16
    f32 = jnp.float32

    segment_row = segments[0]
    same_image = segment_row[:, None] == segment_row[None, :]
    local_segments = lax.dynamic_slice_in_dim(segment_row, tp_rank * local_len, local_len, 0)
    member = (
        local_segments[:, None] == jnp.arange(SEGS, dtype=jnp.int32)[None, :]
    ).astype(f32)

    def token_keep(keep_row):
        return jnp.sum(member * keep_row.astype(f32), axis=1, keepdims=True)

    def place(part_grad, total_len):
        return lax.dynamic_update_slice_in_dim(
            jnp.zeros((total_len,), f32), part_grad, tp_rank * part_grad.shape[0], 0
        )

    def gather_positions(local_rows):
        return lax.all_gather(local_rows, "tp", axis=0, tiled=True)

    def scatter_positions(partial):
        if tp_size == 2:
            halves = partial.reshape(2, local_len, width)
            away = lax.dynamic_index_in_dim(halves, 1 - tp_rank, 0, keepdims=False)
            mine = lax.dynamic_index_in_dim(halves, tp_rank, 0, keepdims=False)
            arrived = lax.ppermute(away, "tp", [(0, 1), (1, 0)])
            return mine.astype(f32) + arrived.astype(f32)
        return lax.psum_scatter(partial, "tp", scatter_dimension=0, tiled=True).astype(f32)

    packed_full = [
        gather_packed(
            jnp.concatenate(
                [
                    qkv_weight[layer].reshape(shard_rows, qkv_end).astype(bf16),
                    proj_weight[layer].T.astype(bf16),
                    fc1_weight[layer].astype(bf16),
                    fc2_weight[layer].T.astype(bf16),
                ],
                axis=1,
            )
        )
        for layer in range(LAYERS)
    ]
    vector_parts = [norm_gains, biases, fc1_bias[:, None, :]]
    vector_full = lax.all_gather(
        jnp.concatenate([part.reshape(-1) for part in vector_parts]),
        ("rows", "tp"),
        axis=0,
        tiled=False,
    )
    full_vectors = []
    first = 0
    for part in vector_parts:
        taken = vector_full[:, first : first + part.size].reshape((-1,) + part.shape)
        first += part.size
        full_vectors.append(jnp.moveaxis(taken, 0, 2).reshape(part.shape[0], part.shape[1], -1))
    gains_full, biases_full, fc1_bias_full = full_vectors

    def heads(rows):
        return jnp.transpose(rows.reshape(full_len, head_count, HEAD_DIM), (1, 0, 2))

    def unheads(by_head):
        return jnp.transpose(by_head, (1, 0, 2)).reshape(full_len, head_cols)

    def head_mul(a, b, dims):
        return lax.dot_general(a, b, (dims, ((0,), (0,))), preferred_element_type=f32)

    def attention_scores(queries, keys):
        scores = head_mul(queries, keys, ((2,), (2,))) * SCORE_SCALE
        return jnp.where(same_image[None], scores, MASK_FILL)

    stream = block_input[:, 0]
    saved = []
    for layer in range(LAYERS):
        packed = packed_full[layer]
        w_qkv = packed[:, :qkv_end]
        w_proj = packed[:, qkv_end:proj_end]
        w_fc1 = packed[:, proj_end:fc1_end]
        w_fc2 = packed[:, fc1_end:]
        gain = gains_full[layer]
        bias = biases_full[layer]
        in_bias = jnp.concatenate(
            [
                lax.dynamic_slice_in_dim(bias[1], tp_rank * head_cols, head_cols, 0),
                jnp.zeros((head_cols,), f32),
                lax.dynamic_slice_in_dim(bias[2], tp_rank * head_cols, head_cols, 0),
            ]
        )
        up_bias = lax.dynamic_slice_in_dim(fc1_bias_full[layer, 0], tp_rank * ff_cols, ff_cols, 0)
        keep_attn = token_keep(keep_flags[layer, 0])
        keep_mlp = token_keep(keep_flags[layer, 1])
        xhat_one, rstd_one = apply_layer_norm(stream)
        normed_one = gather_positions((xhat_one * gain[0] + bias[0]).astype(bf16))
        joined = (mul(normed_one, w_qkv, ((1,), (0,))) + in_bias).astype(bf16)
        queries = heads(joined[:, :head_cols])
        keys = heads(joined[:, head_cols : 2 * head_cols])
        values = heads(joined[:, 2 * head_cols :])
        scores = attention_scores(queries, keys)
        top = jnp.max(scores, axis=-1, keepdims=True)
        exponent = jnp.exp(scores - top)
        total = jnp.sum(exponent, axis=-1, keepdims=True)
        log_total = top + jnp.log(total)
        probs = (exponent / total).astype(bf16)
        context = unheads(head_mul(probs, values, ((2,), (1,))).astype(bf16))
        attn = scatter_positions(mul(context, w_proj, ((1,), (1,))).astype(bf16)) + bias[3]
        middle = stream + keep_attn * attn / KEEP_RATE
        xhat_two, rstd_two = apply_layer_norm(middle)
        normed_two = gather_positions((xhat_two * gain[1] + bias[4]).astype(bf16))
        hidden_pre = mul(normed_two, w_fc1, ((1,), (0,))) + up_bias
        hidden = (hidden_pre * cumulative(hidden_pre)).astype(bf16)
        mlp = scatter_positions(mul(hidden, w_fc2, ((1,), (1,))).astype(bf16)) + bias[5]
        stream = middle + keep_mlp * mlp / KEEP_RATE
        saved.append(
            (
                (w_qkv, w_proj, w_fc1, w_fc2, gain, keep_attn, keep_mlp),
                (xhat_one, rstd_one, normed_one, queries, keys, values, log_total, context),
                (xhat_two, rstd_two, normed_two, hidden_pre, hidden),
            )
        )

    grad = cotangent[:, 0]
    weight_grads = [None] * LAYERS
    vector_grads = [None] * LAYERS
    for layer in reversed(range(LAYERS)):
        (w_qkv, w_proj, w_fc1, w_fc2, gain, keep_attn, keep_mlp), attn_side, mlp_side = saved[layer]
        xhat_one, rstd_one, normed_one, queries, keys, values, log_total, context = attn_side
        xhat_two, rstd_two, normed_two, hidden_pre, hidden = mlp_side
        mlp_grad = grad * keep_mlp / KEEP_RATE
        fc2_bias_grad = jnp.sum(mlp_grad, axis=0)
        mlp_low = gather_positions(mlp_grad.astype(bf16))
        hidden_grad = mul(mlp_low, w_fc2, ((1,), (0,)))
        pre_grad = (hidden_grad * gelu_slope(hidden_pre)).astype(bf16)
        fc1_bias_grad = jnp.sum(pre_grad.astype(f32), axis=0)
        two_grad = scatter_positions(mul(pre_grad, w_fc1, ((1,), (1,))).astype(bf16))
        gain_two_grad = jnp.sum(two_grad * xhat_two, axis=0)
        shift_two_grad = jnp.sum(two_grad, axis=0)
        middle_grad = grad + norm_backward(two_grad, xhat_two, rstd_two, gain[1])
        attn_grad = middle_grad * keep_attn / KEEP_RATE
        proj_bias_grad = jnp.sum(attn_grad, axis=0)
        attn_low = gather_positions(attn_grad.astype(bf16))
        context_low = heads(mul(attn_low, w_proj, ((1,), (0,))).astype(bf16))
        scores = attention_scores(queries, keys)
        probabilities = jnp.exp(scores - log_total)
        value_grad = head_mul(probabilities.astype(bf16), context_low, ((1,), (1,)))
        prob_grad = head_mul(context_low, values, ((2,), (2,)))
        row_delta = jnp.sum(prob_grad * probabilities, axis=-1, keepdims=True)
        score_grad = (probabilities * (prob_grad - row_delta)).astype(bf16)
        query_grad = head_mul(score_grad, keys, ((2,), (1,))) * SCORE_SCALE
        key_grad = head_mul(score_grad, queries, ((1,), (1,))) * SCORE_SCALE
        joined_grad = jnp.concatenate(
            [unheads(part.astype(bf16)) for part in (query_grad, key_grad, value_grad)], axis=1
        )
        in_bias_grad = jnp.sum(joined_grad.astype(f32), axis=0)
        one_grad = scatter_positions(mul(joined_grad, w_qkv, ((1,), (1,))).astype(bf16))
        gain_one_grad = jnp.sum(one_grad * xhat_one, axis=0)
        shift_one_grad = jnp.sum(one_grad, axis=0)
        grad = middle_grad + norm_backward(one_grad, xhat_one, rstd_one, gain[0])
        weight_grads[layer] = scatter_packed(
            jnp.concatenate(
                [
                    mul(normed_one, joined_grad, ((0,), (0,))).astype(bf16),
                    mul(attn_low, context, ((0,), (0,))).astype(bf16),
                    mul(normed_two, pre_grad, ((0,), (0,))).astype(bf16),
                    mul(mlp_low, hidden, ((0,), (0,))).astype(bf16),
                ],
                axis=1,
            )
        )
        vector_grads[layer] = [
            gain_one_grad,
            gain_two_grad,
            shift_one_grad,
            place(in_bias_grad[:head_cols], width),
            place(in_bias_grad[2 * head_cols :], width),
            proj_bias_grad,
            shift_two_grad,
            fc2_bias_grad,
            place(fc1_bias_grad, ff_cols * tp_size),
        ]

    shares = tp_size * lax.axis_size("rows")
    vector_sum = lax.psum_scatter(
        jnp.concatenate(
            [part.reshape(shares, -1) for layer in vector_grads for part in layer], axis=1
        ),
        ("rows", "tp"),
        scatter_dimension=0,
        tiled=True,
    ).reshape(LAYERS, -1)
    part_len = width // shares
    weight_sum = jnp.stack(weight_grads).astype(f32)
    return (
        stream[:, None],
        grad[:, None],
        weight_sum[:, :, :qkv_end].reshape(LAYERS, shard_rows, 3, head_cols),
        jnp.transpose(weight_sum[:, :, qkv_end:proj_end], (0, 2, 1)),
        weight_sum[:, :, proj_end:fc1_end],
        jnp.transpose(weight_sum[:, :, fc1_end:], (0, 2, 1)),
        vector_sum[:, : 2 * part_len].reshape(LAYERS, 2, part_len),
        vector_sum[:, 2 * part_len : 8 * part_len].reshape(LAYERS, 6, part_len),
        vector_sum[:, 8 * part_len :],
    )


def solution(mesh):
    placed = (
        P("tp", "rows", None),
        P("tp", "rows", None),
        P(None, "rows", None, "tp"),
        P(None, "tp", "rows"),
        P(None, "rows", "tp"),
        P(None, "tp", "rows"),
        P(None, None, ("rows", "tp")),
        P(None, None, ("rows", "tp")),
        P(None, ("rows", "tp")),
        P("rows", None),
        P(None, None, "rows", None),
    )
    return jax.shard_map(
        per_device,
        mesh=mesh,
        in_specs=placed,
        out_specs=placed[:2] + placed[2:9],
        check_vma=False,
    )
```

time: 2000 us -> 740 us (0.37)
  waiting for transfers between devices: 1420 us -> 500 us
  blocking collectives: 299 us -> 20.9 us
  local copies, waits for them, and re-layouts: 109 us -> 65.4 us
  matrix products: 103 us -> 75.9 us
    reduce_scatter x16 -> x2, waiting for transfers between devices: 1130 us -> 174 us  [scatter_packed(): return lax.psum_scatter(partial, 'rows', scatter_dimension=0, tiled=True)]
    all_gather x14 -> x8, blocking collectives: 261 us -> 20.9 us  [gather_positions(): return lax.all_gather(local_rows, 'tp', axis=0, tiled=True)]
    unnamed x24 -> x8, waiting for transfers between devices: 89.3 us -> 325 us
    all_gather x6 -> x2, waiting for transfers between devices: 195 us -> 0.01 us  [gather_packed(): return lax.all_gather(shard, 'rows', axis=0, tiled=True)]
    slice x20 -> x34, local copies, waits for them, and re-layouts: 52.1 us -> 6.58 us  [the longest x2 1.5 us: per_device(): queries = heads(joined[:, :head_cols])]
    unnamed x1 -> x0, blocking collectives: 37.9 us -> none
    dot_general x36, matrix products: 103 us -> 75.9 us  [the longest x24 61.3 us: mul(): lax.dot_general(a, b, (dims, ((), ())), preferred_element_type=jnp.float32)]
  transfers between devices with their start and end apart: 23 -> 14, of which waited for: 18 -> 5; matrix products, arithmetic and copies ran while one was open for 8% -> 13% of each run, Pallas kernels for 0% -> 0%
where the time goes in v1:
time: 740 us; the launch traced here: 731 us
  waiting for transfers between devices  500 us (68%)
  matrix products  75.9 us (10%)
  local copies, waits for them, and re-layouts  65.4 us (9%)
  other arithmetic  48 us (6%)
  blocking collectives  20.9 us (3%)
  between operations  18.2 us (2%)
    unnamed x8, waiting for transfers between devices  325 us
    reduce_scatter x2, waiting for transfers between devices, scatter_packed(): return lax.psum_scatter(partial, 'rows', scatter_dimension=0, tiled=True)  174 us
    dot_general x24, matrix products, mul(): lax.dot_general(a, b, (dims, ((), ())), preferred_element_type=jnp.float32)  61.3 us
    all_gather x8, blocking collectives, gather_positions(): return lax.all_gather(local_rows, 'tp', axis=0, tiled=True)  20.9 us
    unnamed x270, local copies, waits for them, and re-layouts  18.4 us
  transfers between devices with their start and end apart: 14, of which 5 were waited for; matrix products, arithmetic and copies ran while one was open for 13% of the time, Pallas kernels for 0%

profile of v1, /device:TPU:0, one launch (start us, length us, event | category | flops | bytes accessed | tf_op | source)
XLA Modules:
  0.0 731.2 jit_solution(13883918422593954156)
XLA Ops:
  18.7 211.5 %all-reduce.5.cloned.1.call-done = f32[18432]{0:T(1024)} async-done(((f32[18432]{0:T(1024)}), f32[18432]{0:T(1024)}) %all-reduce.5.cloned.1.call-update) | async-done | bytes 73744
  234.9 3.5 all_gather.38
  239.3 2.7 fusion.22
  254.8 2.6 all_gather.40
  257.4 5.3 multiply_convert_fusion.3
  262.7 3.6 fusion.45
  280.2 2.7 fusion.23
  296.0 2.8 all_gather.43
  300.5 3.2 convert_reduce_fusion
  303.7 2.8 convolution_convert_fusion.1
  315.9 4.6 convolution_convert_fusion
  322.8 3.2 fusion.89
  326.1 2.5 all_gather.45
  337.7 3.6 fusion.57
  349.9 2.6 convert_reduce_fusion.1
  359.6 4.2 convolution_convert_fusion.2
  385.9 2.7 fusion.54
  402.3 5.7 pad_maximum_fusion.1
  409.1 4.4 convolution_convert_fusion.3
  413.6 2.8 convolution_convert_fusion.4
  419.8 3.4 pad_maximum_fusion
  428.3 113.0 %all-reduce.7.cloned.1.call-done = f32[32,576]{1,0:T(8,128)} async-done(((f32[32,576]{1,0:T(8,128)}), f32[32,576]{1,0:T(8,128)}) %all-reduce.7.cloned.1.call-update) | async-done | bytes 73744
  544.1 17.4 %reduce-scatter.5.cloned.1.call-done = bf16[48,4608]{1,0:T(8,128)(2,1)} async-done(((bf16[768,4608]{1,0:T(8,128)(2,1)}), bf16[48,4608]{1,0:T(8,128)(2,1)}) %reduce-scatter.5.cloned.1.call-update) | async-done | bytes 442384 | tf_op jit(solution)/shard_map/reduce_scatter | solution.py:53
  561.5 157.0 %reduce-scatter.3.cloned.1.call-done = bf16[48,4608]{1,0:T(8,128)(2,1)} async-done(((bf16[768,4608]{1,0:T(8,128)(2,1)}), bf16[48,4608]{1,0:T(8,128)(2,1)}) %reduce-scatter.3.cloned.1.call-update) | async-done | bytes 442384 | tf_op jit(solution)/shard_map/reduce_scatter | solution.py:53
  (507 shorter events, 145.4 us)
Async XLA Ops:
  8.0 222.2 %all-reduce.5.cloned.1.call-start = ((), (), s32[]{:S(2)}) async-start(), calls=%async_computation.6 | async-start | bytes 147456
  11.3 227.1 %all-gather.4.cloned.1.call-start = ((), (), s32[]{:S(2)}) async-start(), calls=%async_computation.2 | async-start | bytes 7520256 | tf_op jit(solution)/shard_map/all_gather | solution.py:49
  15.6 263.7 %all-gather.6.cloned.1.call-start = ((), (), s32[]{:S(2)}) async-start(), calls=%async_computation.3 | async-start | bytes 7520256 | tf_op jit(solution)/shard_map/all_gather | solution.py:49
  16.6 524.7 %all-reduce.7.cloned.1.call-start = ((), (), s32[]{:S(2)}) async-start(), calls=%async_computation.7 | async-start | bytes 163840
  17.7 224.3 %copy-start.82 = (f32[256]{0:T(256)}, f32[256]{0:T(256)S(1)}, u32[]{:S(2)}) copy-start(f32[256]{0:T(256)S(1)} %broadcast_multiply_fusion.11) | copy-start | bytes 3076
  17.9 220.5 %copy-start.104 = (f32[256]{0:T(256)}, f32[256]{0:T(256)S(1)}, u32[]{:S(2)}) copy-start(f32[256]{0:T(256)S(1)} %add_rsqrt_fusion.3) | copy-start | bytes 3076
  250.4 1.9 collective-permute-start
  254.3 20.7 %copy-start.3 = (f32[256,768]{1,0:T(8,128)}, f32[256,768]{1,0:T(8,128)S(1)}, u32[]{:S(2)}) copy-start(f32[256,768]{1,0:T(8,128)S(1)} %get-tuple-element.89) | copy-start | bytes 2359300
  267.2 7.8 %collective-permute-start.1 = (bf16[256,768]{1,0:T(8,128)(2,1)}, bf16[256,768]{1,0:T(8,128)(2,1)}, u32[]{:S(2)}, u32[]{:S(2)}) collective-permute-start(bf16[256,768]{1,0:T(8,128)(2,1)} %dynamic-slice_bitcast_fusion.6), channel_id=1, source_target_pairs={{0,1},{1,0},{2,3},{3,2},{4,5},{5,4},{6,7},{7,6},{8,9},{9,8},{10,11... | collective-permute-start | bytes 1179656 | tf_op jit(solution)/shard_map/ppermute | solution.py:107
  293.0 1.8 collective-permute-start.2
  307.9 12.6 %copy-start.24 = (bf16[512,768]{1,0:T(8,128)(2,1)}, bf16[512,768]{1,0:T(8,128)(2,1)S(1)}, u32[]{:S(2)}) copy-start(bf16[512,768]{1,0:T(8,128)(2,1)S(1)} %fusion.48) | copy-start | bytes 2359300
  308.8 11.7 %collective-permute-start.4 = (bf16[256,768]{1,0:T(8,128)(2,1)}, bf16[256,768]{1,0:T(8,128)(2,1)}, u32[]{:S(2)}, u32[]{:S(2)}) collective-permute-start(bf16[256,768]{1,0:T(8,128)(2,1)} %dynamic-slice_bitcast_fusion.3), channel_id=1, source_target_pairs={{0,1},{1,0},{2,3},{3,2},{4,5},{5,4},{6,7},{7,6},{8,9},{9,8},{10,11... | collective-permute-start | bytes 1179656 | tf_op jit(solution)/shard_map/ppermute | solution.py:107
  315.6 7.1 collective-permute-start.3
  315.9 14.6 %slice-start.2 = ((s8[6291456]{0:T(1024)(128)(4,1)}), s8[4194304]{0:T(1024)(128)(4,1)S(1)}, s32[]{:S(2)}) async-start(s8[6291456]{0:T(1024)(128)(4,1)} %bitcast.275), calls=%async_computation.10 | async-start | bytes 8388608
  336.7 13.1 %slice-start.4 = ((s8[7077888]{0:T(1024)(128)(4,1)}), s8[4194304]{0:T(1024)(128)(4,1)S(1)}, s32[]{:S(2)}) async-start(s8[7077888]{0:T(1024)(128)(4,1)} %bitcast.348), calls=%async_computation.12 | async-start | bytes 8388608
  337.7 12.2 %slice-start.5 = ((s8[7077888]{0:T(1024)(128)(4,1)}), s8[2883584]{0:T(1024)(128)(4,1)S(1)}, s32[]{:S(2)}) async-start(s8[7077888]{0:T(1024)(128)(4,1)} %bitcast.348), calls=%async_computation.13 | async-start | bytes 5767168
  341.4 1.9 collective-permute-start.5
  355.6 11.1 %collective-permute-start.6 = (bf16[256,768]{1,0:T(8,128)(2,1)}, bf16[256,768]{1,0:T(8,128)(2,1)}, u32[]{:S(2)}, u32[]{:S(2)}) collective-permute-start(bf16[256,768]{1,0:T(8,128)(2,1)} %dynamic-slice_bitcast_fusion.1), channel_id=1, source_target_pairs={{0,1},{1,0},{2,3},{3,2},{4,5},{5,4},{6,7},{7,6},{8,9},{9,8},{10,11... | collective-permute-start | bytes 1179656 | tf_op jit(solution)/shard_map/ppermute | solution.py:107
  359.6 17.0 %slice-start = ((s8[6291456]{0:T(1024)(128)(4,1)}), s8[2097152]{0:T(1024)(128)(4,1)S(1)}, s32[]{:S(2)}) async-start(s8[6291456]{0:T(1024)(128)(4,1)} %bitcast.273), calls=%async_computation.8 | async-start | bytes 4194304
  388.6 13.7 %copy-start.19 = (bf16[768,384]{1,0:T(8,128)(2,1)S(1)}, bf16[768,384]{1,0:T(8,128)(2,1)}, u32[]{:S(2)}) copy-start(bf16[768,384]{1,0:T(8,128)(2,1)} %convolution_convert_fusion.9) | copy-start | bytes 1769476
  388.6 13.7 %copy-start.22 = (bf16[768,1152]{1,0:T(8,128)(2,1)S(1)}, bf16[768,1152]{1,0:T(8,128)(2,1)}, u32[]{:S(2)}) copy-start(bf16[768,1152]{1,0:T(8,128)(2,1)} %convolution_convert_fusion.2) | copy-start | bytes 5308420
  390.2 6.9 collective-permute-start.7
  402.2 159.3 %reduce-scatter.5.cloned.1.call-start = ((), (), s32[]{:S(2)}) async-start(), calls=%async_computation.5 | async-start | bytes 7520256 | tf_op jit(solution)/shard_map/reduce_scatter | solution.py:53
  408.0 310.5 %reduce-scatter.3.cloned.1.call-start = ((), (), s32[]{:S(2)}) async-start(), calls=%async_computation.4 | async-start | bytes 7520256 | tf_op jit(solution)/shard_map/reduce_scatter | solution.py:53
  (122 other events, 532.3 us)
Sparse Core Ops, SparseCore 0:
  15.0 215.1 all-reduce.4
  402.4 138.8 all-reduce.6
Sparse Core Ops, SparseCore 1:
  15.7 103.1 all-gather.3
  122.1 99.2 all-gather.5
  408.1 153.4 reduce-scatter.4
  566.9 151.6 reduce-scatter.2

commit v2 on v1

--- a/solution.py
+++ b/solution.py
@@ -1,10 +1,16 @@
+import functools
 import math
 
 import jax
 import jax.numpy as jnp
 from jax import lax
+from jax.experimental import pallas as pl
+from jax.experimental.pallas import tpu as pltpu
 from jax.sharding import PartitionSpec as P
 
+MESH = pl.DeviceIdType.MESH
+LANES = 128
+GATHER_ORDERS = ("zyx", "zxy", "xyz")
 HEAD_DIM = 64
 LAYERS = 2
 SEGS = 8
@@ -45,12 +51,498 @@
     return lax.dot_general(a, b, (dims, ((), ())), preferred_element_type=jnp.float32)
 
 
-def gather_packed(shard):
-    return lax.all_gather(shard, "rows", axis=0, tiled=True)
-
-
-def scatter_packed(partial):
-    return lax.psum_scatter(partial, "rows", scatter_dimension=0, tiled=True)
+def split_columns(total):
+    groups = total // LANES
+    first = groups * 14 // 36
+    return (
+        (0, first * LANES),
+        (first * LANES, first * LANES),
+        (2 * first * LANES, (groups - 2 * first) * LANES),
+    )
+
+
+def places(nz):
+    me = lax.axis_index("rows")
+    px = lax.rem(me, 2)
+    py = lax.rem(lax.div(me, 2), 2)
+    pz = lax.div(me, 4)
+    hops = {
+        "x": me + 1 - 2 * px,
+        "y": me + 2 - 4 * py,
+        "u": lax.min(me + 4, 4 * nz - 1),
+        "d": lax.max(me - 4, 0),
+    }
+    return me, px, py, pz, hops
+
+
+def guarded(cond, act):
+    if cond is None:
+        act()
+    else:
+        pl.when(cond)(act)
+
+
+def both(a, b):
+    if a is None:
+        return b
+    if b is None:
+        return a
+    return jnp.logical_and(a, b)
+
+
+def greet(nz, pz, hops, tp, with_tp):
+    barrier = pltpu.get_barrier_semaphore()
+    ends = {"x": None, "y": None, "u": pz < nz - 1, "d": pz > 0}
+    for name, cond in ends.items():
+        guarded(
+            cond,
+            lambda name=name: pl.semaphore_signal(
+                barrier, inc=1, device_id=(hops[name], tp), device_id_type=MESH
+            ),
+        )
+    waits = 2
+    if with_tp:
+        pl.semaphore_signal(
+            barrier, inc=1, device_id=(lax.axis_index("rows"), 1 - tp), device_id_type=MESH
+        )
+        waits = 3
+    waits = waits + lax.min(pz, 1) + lax.min(nz - 1 - pz, 1)
+    pl.semaphore_wait(barrier, waits)
+    return ends
+
+
+def gather_plan(order, nz):
+    found = []
+    for rx in (0, 1):
+        for ry in (0, 1):
+            for rz in range(1 - nz, nz):
+                rel = {"x": rx, "y": ry, "z": rz}
+                differing = [i for i, dim in enumerate(order) if rel[dim]]
+                last = differing[-1] if differing else -1
+                sends = []
+                if last >= 0 and order[last] == "z":
+                    sends.append("u" if rz < 0 else "d")
+                for dim in order[last + 1 :]:
+                    sends.extend("ud" if dim == "z" else dim)
+                found.append((last + 1, abs(rz), rx + ry, rx, ry, rz, tuple(sends)))
+    return sorted(found)
+
+
+def gather_kernel(nz, layers, rows, cols, shard, vec, full, vec_full, own_sem, recv, send):
+    me, px, py, pz, hops = places(nz)
+    tp = lax.axis_index("tp")
+    n = 4 * nz
+    spans = split_columns(cols)
+    names = "xyud"
+    ends = greet(nz, pz, hops, tp, True)
+
+    def origin(rx, ry, rz):
+        return me + rx * (1 - 2 * px) + ry * 2 * (1 - 2 * py) + 4 * rz
+
+    def block(layer, color, o):
+        start = pl.multiple_of((layer * n + o) * rows, 16)
+        return full.at[pl.ds(start, rows), pl.ds(*spans[color])]
+
+    def copy(layer, color, o, name, own):
+        if color == 3:
+            src = vec_full.at[o]
+            dst = vec_full.at[o]
+        else:
+            dst = block(layer, color, o)
+            src = dst
+            if own:
+                start = pl.multiple_of(layer * rows, 16)
+                src = shard.at[pl.ds(start, rows), pl.ds(*spans[color])]
+        return pltpu.make_async_remote_copy(
+            src_ref=src,
+            dst_ref=dst,
+            send_sem=send.at[layer, color, names.index(name), o],
+            recv_sem=recv.at[layer, color, o],
+            device_id=(hops[name], tp),
+            device_id_type=MESH,
+        )
+
+    keep = pltpu.make_async_copy(vec, vec_full.at[me, tp], own_sem.at[0])
+    keep.start()
+    swap = pltpu.make_async_remote_copy(
+        src_ref=vec,
+        dst_ref=vec_full.at[me, tp],
+        send_sem=own_sem.at[1],
+        recv_sem=own_sem.at[2],
+        device_id=(me, 1 - tp),
+        device_id_type=MESH,
+    )
+    swap.start()
+    plans = [gather_plan(order, nz) for order in GATHER_ORDERS + ("xyz",)]
+
+    def visit(layer, color, item, waiting):
+        _, _, _, rx, ry, rz, sends = item
+        o = origin(rx, ry, rz)
+        own = (rx, ry, rz) == (0, 0, 0)
+        valid = None if rz == 0 else jnp.logical_and(pz + rz >= 0, pz + rz < nz)
+
+        def act():
+            if not waiting and not own:
+                name = "x"
+                copy(layer, color, o, name, False).wait_recv()
+            for name in sends:
+
+                def go(name=name):
+                    c = copy(layer, color, o, name, own)
+                    if waiting:
+                        c.wait_send()
+                    else:
+                        c.start()
+
+                guarded(ends[name], go)
+
+        guarded(valid, act)
+
+    def own_place(layer):
+        src = shard.at[pl.ds(pl.multiple_of(layer * rows, 16), rows), :]
+        dst = full.at[pl.ds(pl.multiple_of((layer * n + me) * rows, 16), rows), :]
+        return pltpu.make_async_copy(src, dst, own_sem.at[3 + layer])
+
+    for phase in range(4):
+        stacks = [[item for item in plan if item[0] == phase] for plan in plans]
+
+        def step(layer, carry):
+            for i in range(max(len(s) for s in stacks[:3])):
+                for color in range(3):
+                    if i < len(stacks[color]):
+                        visit(layer, color, stacks[color][i], False)
+            return carry
+
+        lax.fori_loop(0, layers, step, 0)
+        if phase == 0:
+            lax.fori_loop(0, layers, lambda layer, c: (own_place(layer).start(), c)[1], 0)
+            keep.wait()
+            swap.wait()
+        for item in stacks[3]:
+            visit(0, 3, item, False)
+
+    def finish(layer, carry):
+        for color in range(3):
+            for item in plans[color]:
+                visit(layer, color, item, True)
+        own_place(layer).wait()
+        return carry
+
+    lax.fori_loop(0, layers, finish, 0)
+    for item in plans[3]:
+        visit(0, 3, item, True)
+
+
+def gather_rows(shards, vec, nz):
+    layers, rows, cols = shards.shape
+    n = 4 * nz
+    any_space = pl.BlockSpec(memory_space=pl.ANY)
+    vmem = pl.BlockSpec(memory_space=pltpu.VMEM)
+    full, vec_full = pl.pallas_call(
+        functools.partial(gather_kernel, nz, layers, rows, cols),
+        out_shape=(
+            jax.ShapeDtypeStruct((layers * n * rows, cols), shards.dtype),
+            jax.ShapeDtypeStruct((n, 2) + vec.shape, vec.dtype),
+        ),
+        in_specs=[vmem, vmem],
+        out_specs=(any_space, any_space),
+        scratch_shapes=[
+            pltpu.SemaphoreType.DMA((3 + layers,)),
+            pltpu.SemaphoreType.DMA((layers, 4, n)),
+            pltpu.SemaphoreType.DMA((layers, 4, 4, n)),
+        ],
+        compiler_params=pltpu.CompilerParams(
+            collective_id=0, has_side_effects=True, vmem_limit_bytes=8 * 1024 * 1024
+        ),
+        name="gather_rows",
+    )(shards.reshape(layers * rows, cols), vec)
+    return full.reshape(layers, n * rows, cols), vec_full
+
+
+def sum_kernel(nz, layers, rows, cols, part, out, ra, rb, rc, ry_c, rx_c, sc, send, recv):
+    me, px, py, pz, hops = places(nz)
+    tp = lax.axis_index("tp")
+    n = 4 * nz
+    spans = split_columns(cols)
+    ends = greet(nz, pz, hops, tp, False)
+    base = (0, 5 * nz, 10 * nz)
+    pools = (ra, rb)
+    coord = {"x": px, "y": py}
+    stride = {"x": 1, "y": 2}
+    zs = []
+    for k in range((nz + 1) // 2):
+        zs.extend([nz - 1 - k, k] if nz - 1 - k != k else [k])
+
+    def mine(layer, o, color, count=1):
+        start = pl.multiple_of((layer * n + o) * rows, 16)
+        return part.at[pl.ds(start, count * rows), pl.ds(*spans[color])]
+
+    def copy(src, dst, layer, index, name):
+        return pltpu.make_async_remote_copy(
+            src_ref=src,
+            dst_ref=dst,
+            send_sem=send.at[layer, index],
+            recv_sem=recv.at[layer, index],
+            device_id=(hops[name], tp),
+            device_id_type=MESH,
+        )
+
+    def add(dst, sources, count=rows):
+        def chunk(i, carry):
+            at = pl.ds(pl.multiple_of(i * 16, 16), 16)
+            total = sources[0][at, :].astype(jnp.float32)
+            for s in sources[1:]:
+                total = total + s[at, :].astype(jnp.float32)
+            dst[at, :] = total.astype(dst.dtype)
+            return carry
+
+        lax.fori_loop(0, count // 16, chunk, 0)
+
+    def over_layers(act):
+        lax.fori_loop(0, layers, lambda layer, c: (act(layer), c)[1], 0)
+
+    dims = (("x", "y"), ("y", "x"))
+
+    def dest(color, flip_one, flip_two, z):
+        d1, d2 = dims[color]
+        c1 = coord[d1] if not flip_one else 1 - coord[d1]
+        c2 = coord[d2] if not flip_two else 1 - coord[d2]
+        return 4 * z + stride[d1] * c1 + stride[d2] * c2
+
+    def hop_one(layer, color, flip_two, z):
+        slot = flip_two * nz + z
+        dst = pools[color].at[layer, slot]
+        return copy(
+            mine(layer, dest(color, 1, flip_two, z), color),
+            dst,
+            layer,
+            base[color] + slot,
+            dims[color][0],
+        )
+
+    def hop_two(layer, color, z):
+        pool = pools[color]
+        slot = 2 * nz + z
+        return copy(
+            pool.at[layer, nz + z], pool.at[layer, slot], layer, base[color] + slot, dims[color][1]
+        )
+
+    def line(layer, color, z, name):
+        pool = pools[color]
+        slot = (3 if name == "u" else 4) * nz + z
+        return copy(
+            pool.at[layer, 2 * nz + z], pool.at[layer, slot], layer, base[color] + slot, name
+        )
+
+    def line_c(layer, z, name, direct):
+        slot = (0 if name == "u" else nz) + z
+        dst = rc.at[layer, slot]
+        src = mine(layer, 4 * z, 2, 4) if direct else dst
+        return copy(src, dst, layer, base[2] + slot, name)
+
+    def swap_y(layer):
+        src = sc.at[layer, pl.ds(pl.multiple_of((1 - py) * 2 * rows, 16), 2 * rows), :]
+        return copy(src, ry_c.at[layer], layer, base[2] + 2 * nz, "y")
+
+    def swap_x(layer):
+        src = ry_c.at[layer, pl.ds(pl.multiple_of((1 - px) * rows, 16), rows), :]
+        return copy(src, rx_c.at[layer], layer, base[2] + 2 * nz + 1, "x")
+
+    def start_all(layer):
+        for z in zs:
+            for color in range(2):
+                hop_one(layer, color, 1, z).start()
+            if z > 0:
+                pl.when(pz == 0)(lambda z=z: line_c(layer, z, "u", True).start())
+            if z < nz - 1:
+                pl.when(pz == nz - 1)(lambda z=z: line_c(layer, z, "d", True).start())
+        for z in zs:
+            for color in range(2):
+                hop_one(layer, color, 0, z).start()
+
+    def relay_c(layer, z):
+        if z > 1:
+
+            @pl.when(jnp.logical_and(pz > 0, pz < z))
+            def _():
+                c = line_c(layer, z, "u", False)
+                c.wait_recv()
+                add(rc.at[layer, z], (mine(layer, 4 * z, 2, 4), rc.at[layer, z]), 4 * rows)
+                c.start()
+
+        if z < nz - 2:
+
+            @pl.when(jnp.logical_and(pz < nz - 1, pz > z))
+            def _():
+                c = line_c(layer, z, "d", False)
+                c.wait_recv()
+                at = rc.at[layer, nz + z]
+                add(at, (mine(layer, 4 * z, 2, 4), at), 4 * rows)
+                c.start()
+
+    def second(layer):
+        for z in zs:
+            for color in range(2):
+                hop_one(layer, color, 1, z).wait_recv()
+                at = pools[color].at[layer, nz + z]
+                add(at, (mine(layer, dest(color, 0, 1, z), color), at))
+                hop_two(layer, color, z).start()
+            relay_c(layer, z)
+
+    def settle_c(layer):
+        up = line_c(layer, pz, "u", False)
+        down = line_c(layer, pz, "d", False)
+        own = mine(layer, 4 * pz, 2, 4)
+        from_up = rc.at[layer, pz]
+        from_down = rc.at[layer, nz + pz]
+        target = sc.at[layer]
+
+        @pl.when(pz == 0)
+        def _():
+            down.wait_recv()
+            add(target, (own, from_down), 4 * rows)
+
+        @pl.when(pz == nz - 1)
+        def _():
+            up.wait_recv()
+            add(target, (own, from_up), 4 * rows)
+
+        @pl.when(jnp.logical_and(pz > 0, pz < nz - 1))
+        def _():
+            down.wait_recv()
+            up.wait_recv()
+            add(target, (own, from_up, from_down), 4 * rows)
+
+        swap_y(layer).start()
+
+    def third(layer):
+        for z in zs:
+            for color in range(2):
+                pool = pools[color]
+                hop_one(layer, color, 0, z).wait_recv()
+                hop_two(layer, color, z).wait_recv()
+                at = pool.at[layer, 2 * nz + z]
+                add(at, (mine(layer, dest(color, 0, 0, z), color), pool.at[layer, z], at))
+                pl.when(jnp.logical_and(pz == 0, z > pz))(
+                    lambda c=color, z=z: line(layer, c, z, "u").start()
+                )
+                pl.when(jnp.logical_and(pz == nz - 1, z < pz))(
+                    lambda c=color, z=z: line(layer, c, z, "d").start()
+                )
+
+    def relay(layer):
+        for z in zs:
+            for color in range(2):
+                pool = pools[color]
+                at = pool.at[layer, 2 * nz + z]
+
+                @pl.when(jnp.logical_and(pz > 0, pz < z))
+                def _():
+                    c = line(layer, color, z, "u")
+                    c.wait_recv()
+                    add(at, (at, pool.at[layer, 3 * nz + z]))
+                    c.start()
+
+                @pl.when(jnp.logical_and(pz < nz - 1, pz > z))
+                def _():
+                    c = line(layer, color, z, "d")
+                    c.wait_recv()
+                    add(at, (at, pool.at[layer, 4 * nz + z]))
+                    c.start()
+
+    def out_at(layer, color):
+        return out.at[pl.ds(pl.multiple_of(layer * rows, 16), rows), pl.ds(*spans[color])]
+
+    def x_c(layer):
+        swap_y(layer).wait_recv()
+        own = sc.at[layer, pl.ds(pl.multiple_of(py * 2 * rows, 16), 2 * rows), :]
+        add(ry_c.at[layer], (own, ry_c.at[layer]), 2 * rows)
+        swap_x(layer).start()
+
+    def final(layer):
+        for color in range(2):
+            pool = pools[color]
+            up = line(layer, color, pz, "u")
+            down = line(layer, color, pz, "d")
+            own = pool.at[layer, 2 * nz + pz]
+            from_up = pool.at[layer, 3 * nz + pz]
+            from_down = pool.at[layer, 4 * nz + pz]
+            target = out_at(layer, color)
+
+            @pl.when(pz == 0)
+            def _():
+                down.wait_recv()
+                add(target, (own, from_down))
+
+            @pl.when(pz == nz - 1)
+            def _():
+                up.wait_recv()
+                add(target, (own, from_up))
+
+            @pl.when(jnp.logical_and(pz > 0, pz < nz - 1))
+            def _():
+                down.wait_recv()
+                up.wait_recv()
+                add(target, (own, from_up, from_down))
+
+        swap_x(layer).wait_recv()
+        own = ry_c.at[layer, pl.ds(pl.multiple_of(px * rows, 16), rows), :]
+        add(out_at(layer, 2), (own, rx_c.at[layer]))
+
+    def drain(layer):
+        for z in zs:
+            for color in range(2):
+                hop_one(layer, color, 1, z).wait_send()
+                hop_one(layer, color, 0, z).wait_send()
+                hop_two(layer, color, z).wait_send()
+                pl.when(pz < z)(lambda c=color, z=z: line(layer, c, z, "u").wait_send())
+                pl.when(pz > z)(lambda c=color, z=z: line(layer, c, z, "d").wait_send())
+            pl.when(pz < z)(lambda z=z: line_c(layer, z, "u", False).wait_send())
+            pl.when(pz > z)(lambda z=z: line_c(layer, z, "d", False).wait_send())
+        swap_y(layer).wait_send()
+        swap_x(layer).wait_send()
+
+    for act in (start_all, second, settle_c, third, x_c, relay, final, drain):
+        over_layers(act)
+
+
+def sum_rows(parts, nz):
+    layers, depth, cols = parts.shape
+    n = 4 * nz
+    rows = depth // n
+    spans = split_columns(cols)
+    vmem = pl.BlockSpec(memory_space=pltpu.VMEM)
+    dt = parts.dtype
+    count = 12 * nz + 2
+    out = pl.pallas_call(
+        functools.partial(sum_kernel, nz, layers, rows, cols),
+        out_shape=jax.ShapeDtypeStruct((layers * rows, cols), jnp.float32),
+        in_specs=[vmem],
+        out_specs=vmem,
+        scratch_shapes=[
+            pltpu.VMEM((layers, 5 * nz, rows, spans[0][1]), dt),
+            pltpu.VMEM((layers, 5 * nz, rows, spans[1][1]), dt),
+            pltpu.VMEM((layers, 2 * nz, 4 * rows, spans[2][1]), dt),
+            pltpu.VMEM((layers, 2 * rows, spans[2][1]), dt),
+            pltpu.VMEM((layers, rows, spans[2][1]), dt),
+            pltpu.VMEM((layers, 4 * rows, spans[2][1]), dt),
+            pltpu.SemaphoreType.DMA((layers, count)),
+            pltpu.SemaphoreType.DMA((layers, count)),
+        ],
+        compiler_params=pltpu.CompilerParams(
+            collective_id=1, has_side_effects=True, vmem_limit_bytes=60 * 1024 * 1024
+        ),
+        name="sum_rows",
+    )(parts.reshape(layers * depth, cols))
+    return out.reshape(layers, rows, cols)
+
+
+def pair_sum(rows, tp_rank):
+    layers, depth, cols = rows.shape
+    halves = rows.reshape(layers, 2, depth // 2, cols)
+    away = lax.dynamic_index_in_dim(halves, 1 - tp_rank, 1, keepdims=False)
+    mine = lax.dynamic_index_in_dim(halves, tp_rank, 1, keepdims=False)
+    return mine + lax.ppermute(away, "tp", [(0, 1), (1, 0)])
 
 
 def per_device(
@@ -108,8 +600,10 @@
             return mine.astype(f32) + arrived.astype(f32)
         return lax.psum_scatter(partial, "tp", scatter_dimension=0, tiled=True).astype(f32)
 
-    packed_full = [
-        gather_packed(
+    row_devices = lax.axis_size("rows")
+    own_kernels = shard_rows % 16 == 0 and row_devices % 4 == 0 and tp_size == 2
+    shards = jnp.stack(
+        [
             jnp.concatenate(
                 [
                     qkv_weight[layer].reshape(shard_rows, qkv_end).astype(bf16),
@@ -119,16 +613,22 @@
                 ],
                 axis=1,
             )
-        )
-        for layer in range(LAYERS)
-    ]
+            for layer in range(LAYERS)
+        ]
+    )
     vector_parts = [norm_gains, biases, fc1_bias[:, None, :]]
-    vector_full = lax.all_gather(
-        jnp.concatenate([part.reshape(-1) for part in vector_parts]),
-        ("rows", "tp"),
-        axis=0,
-        tiled=False,
-    )
+    vector_flat = jnp.concatenate([part.reshape(-1) for part in vector_parts])
+    if own_kernels:
+        filled = -(-vector_flat.size // (8 * LANES)) * 8 * LANES
+        packed_full, vector_full = gather_rows(
+            shards,
+            jnp.pad(vector_flat, (0, filled - vector_flat.size)).reshape(-1, LANES),
+            row_devices // 4,
+        )
+        vector_full = vector_full.reshape(row_devices * tp_size, -1)
+    else:
+        packed_full = lax.all_gather(shards, "rows", axis=1, tiled=True)
+        vector_full = lax.all_gather(vector_flat, ("rows", "tp"), axis=0, tiled=False)
     full_vectors = []
     first = 0
     for part in vector_parts:
@@ -201,7 +701,6 @@
 
     grad = cotangent[:, 0]
     weight_grads = [None] * LAYERS
-    vector_grads = [None] * LAYERS
     for layer in reversed(range(LAYERS)):
         (w_qkv, w_proj, w_fc1, w_fc2, gain, keep_attn, keep_mlp), attn_side, mlp_side = saved[layer]
         xhat_one, rstd_one, normed_one, queries, keys, values, log_total, context = attn_side
@@ -236,50 +735,52 @@
         gain_one_grad = jnp.sum(one_grad * xhat_one, axis=0)
         shift_one_grad = jnp.sum(one_grad, axis=0)
         grad = middle_grad + norm_backward(one_grad, xhat_one, rstd_one, gain[0])
-        weight_grads[layer] = scatter_packed(
-            jnp.concatenate(
-                [
-                    mul(normed_one, joined_grad, ((0,), (0,))).astype(bf16),
-                    mul(attn_low, context, ((0,), (0,))).astype(bf16),
-                    mul(normed_two, pre_grad, ((0,), (0,))).astype(bf16),
-                    mul(mlp_low, hidden, ((0,), (0,))).astype(bf16),
-                ],
-                axis=1,
-            )
-        )
-        vector_grads[layer] = [
-            gain_one_grad,
-            gain_two_grad,
-            shift_one_grad,
-            place(in_bias_grad[:head_cols], width),
-            place(in_bias_grad[2 * head_cols :], width),
-            proj_bias_grad,
-            shift_two_grad,
-            fc2_bias_grad,
-            place(fc1_bias_grad, ff_cols * tp_size),
+        columns = [
+            gain_one_grad[:, None],
+            gain_two_grad[:, None],
+            shift_one_grad[:, None],
+            place(in_bias_grad[:head_cols], width)[:, None],
+            place(in_bias_grad[2 * head_cols :], width)[:, None],
+            proj_bias_grad[:, None],
+            shift_two_grad[:, None],
+            fc2_bias_grad[:, None],
+            place(fc1_bias_grad, ff_cols * tp_size).reshape(width, -1),
         ]
-
-    shares = tp_size * lax.axis_size("rows")
+        filler = LANES - sum(part.shape[1] for part in columns)
+        columns.append(jnp.zeros((width, filler), f32))
+        weight_grads[layer] = jnp.concatenate(
+            [
+                mul(normed_one, joined_grad, ((0,), (0,))).astype(bf16),
+                mul(attn_low, context, ((0,), (0,))).astype(bf16),
+                mul(normed_two, pre_grad, ((0,), (0,))).astype(bf16),
+                mul(mlp_low, hidden, ((0,), (0,))).astype(bf16),
+                jnp.concatenate(columns, axis=1).astype(bf16),
+            ],
+            axis=1,
+        )
+
+    partials = jnp.stack(weight_grads)
+    if own_kernels:
+        weight_sum = sum_rows(partials, row_devices // 4)
+    else:
+        weight_sum = lax.psum_scatter(
+            partials, "rows", scatter_dimension=1, tiled=True
+        ).astype(f32)
+    fc2_end = fc1_end + ff_cols
     vector_sum = lax.psum_scatter(
-        jnp.concatenate(
-            [part.reshape(shares, -1) for layer in vector_grads for part in layer], axis=1
-        ),
-        ("rows", "tp"),
-        scatter_dimension=0,
-        tiled=True,
-    ).reshape(LAYERS, -1)
-    part_len = width // shares
-    weight_sum = jnp.stack(weight_grads).astype(f32)
+        weight_sum[:, :, fc2_end:], "tp", scatter_dimension=1, tiled=True
+    ) if tp_size != 2 else pair_sum(weight_sum[:, :, fc2_end:], tp_rank)
+    vector_rows = jnp.transpose(vector_sum[:, :, :8], (0, 2, 1))
     return (
         stream[:, None],
         grad[:, None],
         weight_sum[:, :, :qkv_end].reshape(LAYERS, shard_rows, 3, head_cols),
         jnp.transpose(weight_sum[:, :, qkv_end:proj_end], (0, 2, 1)),
         weight_sum[:, :, proj_end:fc1_end],
-        jnp.transpose(weight_sum[:, :, fc1_end:], (0, 2, 1)),
-        vector_sum[:, : 2 * part_len].reshape(LAYERS, 2, part_len),
-        vector_sum[:, 2 * part_len : 8 * part_len].reshape(LAYERS, 6, part_len),
-        vector_sum[:, 8 * part_len :],
+        jnp.transpose(weight_sum[:, :, fc1_end:fc2_end], (0, 2, 1)),
+        vector_rows[:, :2],
+        vector_rows[:, 2:8],
+        vector_sum[:, :, 8 : 8 + ff_cols * tp_size // width].reshape(LAYERS, -1),
     )
 
 

time: 740 us -> 519 us (0.70)
  waiting for transfers between devices: 500 us -> 0.02 us
  Pallas kernels: 0 us -> 277 us
  local copies, waits for them, and re-layouts: 65.4 us -> 87.7 us
  between operations: 18.2 us -> 3.18 us
    unnamed x8 -> x0, waiting for transfers between devices: 325 us -> none
    pallas_call x0 -> x2, Pallas kernels: none -> 277 us  [the longest x1 154 us: sum_rows(): pl.pallas_call(functools.partial(sum_kernel, nz, layers, rows, cols), out...]
    reduce_scatter x2 -> x0, waiting for transfers between devices: 174 us -> none  [scatter_packed(): return lax.psum_scatter(partial, 'rows', scatter_dimension=0, tiled=True)]
    concatenate x1 -> x2, local copies, waits for them, and re-layouts: 1.68 us -> 25.2 us  [per_device(): jnp.concatenate([mul(normed_one, joined_grad, ((0,), (0,))).astype(bf16),...]
    reshape x23 -> x5, local copies, waits for them, and re-layouts: 16.1 us -> 3.73 us  [the longest x2 2.91 us: per_device(): place(fc1_bias_grad, ff_cols * tp_size).reshape(width, -1)]
    another operation x4 -> x7, other arithmetic: 3.16 us -> 15.5 us  [the longest x1 13.1 us: per_device(): partials = jnp.stack(weight_grads)]
    concatenate x4 -> x0, other arithmetic: 10.7 us -> none  [the longest x2 9.07 us: per_device(): jnp.concatenate([mul(normed_one, joined_grad, ((0,), (0,))).astype(bf16),...]
    broadcast_in_dim x0 -> x16, local copies, waits for them, and re-layouts: none -> 9.58 us  [the longest x2 1.7 us: per_device(): shift_two_grad[:, None]]
  transfers between devices with their start and end apart: 14 -> 9, of which waited for: 5 -> 0; matrix products, arithmetic and copies ran while one was open for 13% -> 13% of each run, Pallas kernels for 0% -> 0%
where the time goes in v2:
time: 519 us; the launch traced here: 513 us
  Pallas kernels  277 us (53%)
  local copies, waits for them, and re-layouts  87.7 us (17%)
  matrix products  80.6 us (16%)
  other arithmetic  41.5 us (8%)
  blocking collectives  20.5 us (4%)
    pallas_call x1, Pallas kernels, sum_rows(): pl.pallas_call(functools.partial(sum_kernel, nz, layers, rows, cols), out...  154 us
    pallas_call x1, Pallas kernels, gather_rows(): pl.pallas_call(functools.partial(gather_kernel, nz, layers, rows, cols),...  123 us
    dot_general x24, matrix products, mul(): lax.dot_general(a, b, (dims, ((), ())), preferred_element_type=jnp.float32)  66.5 us
    concatenate x2, local copies, waits for them, and re-layouts, per_device(): jnp.concatenate([mul(normed_one, joined_grad, ((0,), (0,))).astype(bf16),...  25.2 us
    all_gather x8, blocking collectives, gather_positions(): return lax.all_gather(local_rows, 'tp', axis=0, tiled=True)  20.5 us
    unnamed x256, local copies, waits for them, and re-layouts  17.5 us
    dot_general x12, matrix products, head_mul(): lax.dot_general(a, b, (dims, ((0,), (0,))), preferred_element_type=f32)  14 us
    another operation x1, other arithmetic, per_device(): partials = jnp.stack(weight_grads)  13.1 us
  transfers between devices with their start and end apart: 9, of which 0 were waited for; matrix products, arithmetic and copies ran while one was open for 13% of the time, Pallas kernels for 0%

profile of v2, /device:TPU:0, one launch (start us, length us, event | category | flops | bytes accessed | tf_op | source)
XLA Modules:
  0.0 512.6 jit_solution(14358325972434132037)
XLA Ops:
  3.8 122.9 %gather_rows.1 = (bf16[1536,4608]{1,0:T(8,128)(2,1)S(1)}, f32[16,2,8,128]{3,2,1,0:T(8,128)S(1)}) custom-call(bf16[96,4608]{1,0:T(8,128)(2,1)S(1)} %bitcast.287, f32[8,128]{1,0:T(8,128)S(1)} %fusion.115.vec), custom_call_target="tpu_custom_call" | custom-call | tf_op jit(solution)/shard_map/gather_rows/pallas_call | solution.py:241
  126.7 5.0 copy-done
  138.3 2.7 fusion.22
  160.1 5.1 %multiply_convert_fusion.3 = (bf16[512,1536]{1,0:T(8,128)(2,1)S(1)}, f32[512,1536]{1,0:T(8,128)}) fusion(f32[1536]{0:T(1024)S(1)} %dynamic_slice.82, bf16[512,768]{1,0:T(8,128)(2,1)S(1)} %all_gather.25, bf16[1536,4608]{1,0:T(8,128)(2,1)} %copy-done), kind=kOutput, calls=%fused_computation.47 | convolution fusion | flops 1212678144 | bytes 7870464 | tf_op jit(solution)/shard_map/dot_general | solution.py:51
  165.3 3.7 fusion.45
  172.1 2.8 all_gather.26
  174.9 3.0 fusion.23
  201.3 3.2 convert_reduce_fusion
  205.9 2.8 convolution_convert_fusion.1
  216.2 4.7 convolution_convert_fusion
  222.6 2.6 fusion.89
  225.3 2.7 all_gather.29
  236.4 2.8 fusion.57
  252.9 4.4 convert_reduce_fusion.1
  257.3 3.7 fusion.42
  263.0 2.8 convolution_convert_fusion.3
  269.7 12.8 %concatenate.41 = bf16[768,4736]{1,0:T(8,128)(2,1)} concatenate(bf16[768,1152]{1,0:T(8,128)(2,1)} %convolution_convert_fusion.2, bf16[768,384]{1,0:T(8,128)(2,1)S(1)} %copy-done.17, bf16[768,1536]{1,0:T(8,128)(2,1)} %convolution_convert_fusion.1, bf16[768,1536]{1,0:T(8,128)(2,1)} %convolution_convert_fusion, bf16[768,1]{1,0:T(8,128)(2,1)} %broadcast_in_dim.157, ...), dimensions={1} | concatenate | bytes 14548992 | tf_op jit(solution)/shard_map/concatenate | solution.py:751
  282.5 4.6 convolution_convert_fusion.4
  291.5 2.6 all_gather.31
  303.5 3.6 fusion.54
  313.0 3.9 convolution_convert_fusion.5
  319.0 12.5 %concatenate.40 = bf16[768,4736]{1,0:T(8,128)(2,1)} concatenate(bf16[768,1152]{1,0:T(8,128)(2,1)} %convolution_convert_fusion.5, bf16[768,384]{1,0:T(8,128)(2,1)S(1)} %copy.127, bf16[768,1536]{1,0:T(8,128)(2,1)} %convolution_convert_fusion.4, bf16[768,1536]{1,0:T(8,128)(2,1)} %convolution_convert_fusion.3, bf16[768,1]{1,0:T(8,128)(2,1)S(1)} %broadcast_in_dim.149, ...), dimensions={1} | concatenate | bytes 14548992 | tf_op jit(solution)/shard_map/concatenate | solution.py:751
  331.5 13.1 %pad_maximum_fusion = bf16[2,768,4736]{2,1,0:T(8,128)(2,1)} fusion(bf16[1,768,4736]{2,1,0:T(8,128)(2,1)} %bitcast.296, bf16[1,768,4736]{2,1,0:T(8,128)(2,1)} %bitcast.297), kind=kLoop, calls=%fused_computation | loop fusion | flops 7274496 | bytes 29097984 | tf_op jit(solution)/shard_map/stack | solution.py:762
  344.6 154.0 %sum_rows.1 = f32[96,4736]{1,0:T(8,128)} custom-call(bf16[1536,4736]{1,0:T(8,128)(2,1)} %bitcast.295), custom_call_target="tpu_custom_call" | custom-call | tf_op jit(solution)/shard_map/sum_rows/pallas_call | solution.py:517
  (477 shorter events, 127.6 us)
Async XLA Ops:
  3.2 130.3 %copy-start.3 = (f32[256,1,768]{2,1,0:T(1,128)S(1)}, f32[256,1,768]{2,1,0:T(1,128)}, u32[]{:S(2)}) copy-start(f32[256,1,768]{2,1,0:T(1,128)} %param.11) | copy-start | bytes 2359300
  147.3 9.4 %copy-start.33 = (bf16[6,512,64]{1,2,0:T(8,128)(2,1)}, bf16[6,512,64]{1,2,0:T(8,128)(2,1)S(1)}, u32[]{:S(2)}) copy-start(bf16[6,512,64]{1,2,0:T(8,128)(2,1)S(1)} %fusion.71) | copy-start | bytes 1179652
  147.3 8.7 %copy-start.109 = (s32[2,2,1,8]{3,2,1,0:T(1,128)S(1)}, s32[2,2,1,8]{3,2,1,0:T(1,128)}, u32[]{:S(2)}) copy-start(s32[2,2,1,8]{3,2,1,0:T(1,128)} %param.21) | copy-start | bytes 388
  149.1 7.5 %collective-permute-start = (bf16[256,768]{1,0:T(8,128)(2,1)S(1)}, bf16[256,768]{1,0:T(8,128)(2,1)S(1)}, u32[]{:S(2)}, u32[]{:S(2)}) collective-permute-start(bf16[256,768]{1,0:T(8,128)(2,1)S(1)} %dynamic-slice_bitcast_fusion.7), channel_id=1, source_target_pairs={{0,1},{1,0},{2,3},{3,2},{4,5},{5,4},{6,7},{7,6},{8,9},{9,8},{10,11... | collective-permute-start | bytes 1179656 | tf_op jit(solution)/shard_map/ppermute | solution.py:599
  156.7 12.8 %copy-start.95 = (f32[256]{0:T(256)}, f32[256]{0:T(256)S(1)}, u32[]{:S(2)}) copy-start(f32[256]{0:T(256)S(1)} %get-tuple-element.62) | copy-start | bytes 3076
  156.7 14.6 %copy-start.82 = (f32[256]{0:T(256)}, f32[256]{0:T(256)S(1)}, u32[]{:S(2)}) copy-start(f32[256]{0:T(256)S(1)} %get-tuple-element.64) | copy-start | bytes 3076
  157.5 7.7 %copy-start.88 = (f32[256]{0:T(256)}, f32[256]{0:T(256)S(1)}, u32[]{:S(2)}) copy-start(f32[256]{0:T(256)S(1)} %add_rsqrt_fusion.2) | copy-start | bytes 3076
  169.0 2.2 collective-permute-start.1
  188.7 7.6 %copy-start.35 = (bf16[6,512,64]{1,2,0:T(8,128)(2,1)}, bf16[6,512,64]{1,2,0:T(8,128)(2,1)S(1)}, u32[]{:S(2)}) copy-start(bf16[6,512,64]{1,2,0:T(8,128)(2,1)S(1)} %fusion.70) | copy-start | bytes 1179652
  188.7 7.6 %copy-start.77 = (f32[768]{0:T(1024)S(1)}, f32[768]{0:T(1024)}, u32[]{:S(2)}) copy-start(f32[768]{0:T(1024)} %add.306) | copy-start | bytes 9220
  192.9 3.4 collective-permute-start.2
  211.0 9.9 %collective-permute-start.4 = (bf16[256,768]{1,0:T(8,128)(2,1)}, bf16[256,768]{1,0:T(8,128)(2,1)}, u32[]{:S(2)}, u32[]{:S(2)}) collective-permute-start(bf16[256,768]{1,0:T(8,128)(2,1)} %dynamic-slice_bitcast_fusion.3), channel_id=1, source_target_pairs={{0,1},{1,0},{2,3},{3,2},{4,5},{5,4},{6,7},{7,6},{8,9},{9,8},{10,11... | collective-permute-start | bytes 1179656 | tf_op jit(solution)/shard_map/ppermute | solution.py:599
  212.2 10.4 %collective-permute-start.3 = (bf16[256,768]{1,0:T(8,128)(2,1)}, bf16[256,768]{1,0:T(8,128)(2,1)}, u32[]{:S(2)}, u32[]{:S(2)}) collective-permute-start(bf16[256,768]{1,0:T(8,128)(2,1)} %dynamic-slice_bitcast_fusion.4), channel_id=1, source_target_pairs={{0,1},{1,0},{2,3},{3,2},{4,5},{5,4},{6,7},{7,6},{8,9},{9,8},{10,11... | collective-permute-start | bytes 1179656 | tf_op jit(solution)/shard_map/ppermute | solution.py:599
  216.2 13.7 %slice-start.6 = ((s8[6291456]{0:T(1024)(128)(4,1)}), s8[4194304]{0:T(1024)(128)(4,1)S(1)}, s32[]{:S(2)}) async-start(s8[6291456]{0:T(1024)(128)(4,1)} %bitcast.293), calls=%async_computation.6 | async-start | bytes 8388608
  220.9 9.0 %slice-start.7 = ((s8[6291456]{0:T(1024)(128)(4,1)}), s8[2097152]{0:T(1024)(128)(4,1)S(1)}, s32[]{:S(2)}) async-start(s8[6291456]{0:T(1024)(128)(4,1)} %bitcast.293), calls=%async_computation.7 | async-start | bytes 4194304
  240.9 7.2 %collective-permute-start.5 = (bf16[256,768]{1,0:T(8,128)(2,1)S(1)}, bf16[256,768]{1,0:T(8,128)(2,1)S(1)}, u32[]{:S(2)}, u32[]{:S(2)}) collective-permute-start(bf16[256,768]{1,0:T(8,128)(2,1)S(1)} %dynamic-slice_bitcast_fusion.2), channel_id=1, source_target_pairs={{0,1},{1,0},{2,3},{3,2},{4,5},{5,4},{6,7},{7,6},{8,9},{9,8},{10,11... | collective-permute-start | bytes 1179656 | tf_op jit(solution)/shard_map/ppermute | solution.py:599
  262.7 24.5 %collective-permute-start.6 = (bf16[256,768]{1,0:T(8,128)(2,1)}, bf16[256,768]{1,0:T(8,128)(2,1)}, u32[]{:S(2)}, u32[]{:S(2)}) collective-permute-start(bf16[256,768]{1,0:T(8,128)(2,1)} %dynamic-slice_bitcast_fusion.1), channel_id=1, source_target_pairs={{0,1},{1,0},{2,3},{3,2},{4,5},{5,4},{6,7},{7,6},{8,9},{9,8},{10,11... | collective-permute-start | bytes 1179656 | tf_op jit(solution)/shard_map/ppermute | solution.py:599
  269.7 12.8 %copy-start.20 = (bf16[768,116]{1,0:T(8,128)(2,1)}, bf16[768,116]{1,0:T(8,128)(2,1)S(1)}, u32[]{:S(2)}) copy-start(bf16[768,116]{1,0:T(8,128)(2,1)S(1)} %broadcast.235) | copy-start | bytes 534532
  282.5 13.3 %slice-start.4 = ((s8[6291456]{0:T(1024)(128)(4,1)}), s8[4194304]{0:T(1024)(128)(4,1)S(1)}, s32[]{:S(2)}) async-start(s8[6291456]{0:T(1024)(128)(4,1)} %bitcast.291), calls=%async_computation.4 | async-start | bytes 8388608
  287.1 8.6 %slice-start.5 = ((s8[6291456]{0:T(1024)(128)(4,1)}), s8[2097152]{0:T(1024)(128)(4,1)S(1)}, s32[]{:S(2)}) async-start(s8[6291456]{0:T(1024)(128)(4,1)} %bitcast.291), calls=%async_computation.5 | async-start | bytes 4194304
  308.5 8.4 %collective-permute-start.7 = (bf16[256,768]{1,0:T(8,128)(2,1)S(1)}, bf16[256,768]{1,0:T(8,128)(2,1)S(1)}, u32[]{:S(2)}, u32[]{:S(2)}) collective-permute-start(bf16[256,768]{1,0:T(8,128)(2,1)S(1)} %dynamic-slice_bitcast_fusion), channel_id=1, source_target_pairs={{0,1},{1,0},{2,3},{3,2},{4,5},{5,4},{6,7},{7,6},{8,9},{9,8},{10,11... | collective-permute-start | bytes 1179656 | tf_op jit(solution)/shard_map/ppermute | solution.py:599
  344.6 158.5 %copy-start.107 = (f32[256]{0:T(256)S(1)}, f32[256]{0:T(256)}, u32[]{:S(2)}) copy-start(f32[256]{0:T(256)} %get-tuple-element.43) | copy-start | bytes 3076
  344.6 158.5 %copy-start.39 = (bf16[256,768]{1,0:T(8,128)(2,1)S(1)}, bf16[256,768]{1,0:T(8,128)(2,1)}, u32[]{:S(2)}) copy-start(bf16[256,768]{1,0:T(8,128)(2,1)} %copy-done.38) | copy-start | bytes 1179652
  503.1 6.1 %collective-permute-start.8 = (f32[2,24,128]{1,0,2:T(2,128)}, f32[2,24,128]{1,0,2:T(2,128)}, u32[]{:S(2)}, u32[]{:S(2)}) collective-permute-start(f32[2,24,128]{1,0,2:T(2,128)} %bitcast.99), channel_id=1, source_target_pairs={{0,1},{1,0},{2,3},{3,2},{4,5},{5,4},{6,7},{7,6},{8,9},{9,8},{10,11... | collective-permute-start | bytes 73736 | tf_op jit(solution)/shard_map/ppermute | solution.py:545
  (109 other events, 444.3 us)
